TPU v7x, 32 devices: a whole 2x2x4 slice. The times are simulated.
32 devices in a mesh: ctx: 8 (over y, x, core), head: 4 (over z).
Axes of the slice: x: 2, y: 2, z: 4, core: 2. Of those that a mesh axis runs over, the one named last changes fastest.
Arguments:
- prompt_values: bfloat16 [4096, 8192], P('ctx', 'head'), may hold values from -6 to 6
- prompt_gate: bfloat16 [4096, 8192], P('ctx', 'head'), may hold values from -6 to 6
- prompt_inject: bfloat16 [4096, 4, 256], P('ctx', 'head'), may hold values from -6 to 6
- prompt_read: bfloat16 [4096, 4, 256], P('ctx', 'head'), may hold values from -0.375 to 0.375
- prompt_step: float32 [128, 4096], P('head', 'ctx'), may hold values from -8 to 256
- decay_log: float32 [128], P('head'), may hold values from -10 to 0
- skip_gain: float32 [128], P('head'), may hold values from 0.5 to 1.5
- norm_weight: float32 [8192], P('head'), may hold values from 0.1 to 1.9
- out_weight: bfloat16 [8192, 4096], P('head'), may hold values from -0.0625 to 0.0625
- sample_values: bfloat16 [16, 16, 8192], P('ctx', None, 'head'), may hold values from -6 to 6
- sample_gate: bfloat16 [16, 16, 8192], P('ctx', None, 'head'), may hold values from -6 to 6
- sample_inject: bfloat16 [16, 16, 4, 256], P('ctx', None, 'head'), may hold values from -6 to 6
- sample_read: bfloat16 [16, 16, 4, 256], P('ctx', None, 'head'), may hold values from -0.375 to 0.375
- sample_step: float32 [128, 16, 16], P('head', 'ctx'), may hold values from -8 to 256
- sample_length: int32 [16], P('ctx'), may hold values from 1 to 16
Outputs:
- prompt_mixed: bfloat16 [4096, 4096], P('head', 'ctx')
- sample_mixed: bfloat16 [4096, 16], P('head', 'ctx')
All inputs are finite; a program needn't handle non-finite values.
Results may differ from a plain program's by a relative error of at most 0.02.
Values may be sent and summed in bfloat16 or wider, within the bound.
A program may use at most 192 MiB of HBM per device.

v0:
```python
import functools

import jax
import jax.numpy as jnp
from jax import lax
from jax.experimental import pallas as pl
from jax.experimental.pallas import tpu as pltpu
from jax.sharding import PartitionSpec as P

BLOCK = 128
LANES = 128
PAD = 8
F32 = jnp.float32
BF16 = jnp.bfloat16
EXACT = lax.Precision.HIGHEST
VMEM_LIMIT = 60 * 1024 * 1024


def dot(a, b, dims=((1,), (0,)), precision=None):
    return lax.dot_general(a, b, (dims, ((), ())), precision=precision, preferred_element_type=F32)


def softplus(v):
    return jnp.maximum(v, 0.0) + jnp.log1p(jnp.exp(-jnp.abs(v)))


def silu(v):
    return v / (1.0 + jnp.exp(-v))


def spread(w, expander):
    high = w.astype(BF16)
    low = (w - high.astype(F32)).astype(BF16)
    return dot(jnp.concatenate([high, low], axis=1), expander)


def expander_of(heads, dim):
    row = lax.broadcasted_iota(jnp.int32, (2 * heads, heads * dim), 0)
    lane = lax.broadcasted_iota(jnp.int32, (2 * heads, heads * dim), 1)
    head = lane // dim
    return jnp.where((row == head) | (row == head + heads), 1.0, 0.0).astype(BF16)


def square(n):
    return (
        lax.broadcasted_iota(jnp.int32, (n, n), 0),
        lax.broadcasted_iota(jnp.int32, (n, n), 1),
    )


def state_kernel(dim, values_ref, inject_ref, step_ref, rate_ref, state_ref, log_ref, scaled_ref):
    tokens, channels = values_ref.shape
    heads = channels // dim
    steps = softplus(step_ref[...])
    logs = steps * rate_ref[...]
    i, j = square(tokens)
    after = dot(jnp.where(j > i, 1.0, 0.0), logs, ((1,), (1,)), EXACT)
    total = dot(jnp.ones((PAD, tokens), F32), logs, ((1,), (1,)), EXACT)
    turned = dot(jnp.where(i == j, 1.0, 0.0), steps, ((1,), (1,)), EXACT)
    weight = jnp.exp(after) * turned
    expander = expander_of(heads, dim)
    for b in range(tokens // BLOCK):
        rows = pl.ds(b * BLOCK, BLOCK)
        wide = spread(weight[b * BLOCK : (b + 1) * BLOCK], expander)
        scaled_ref[rows, :] = (wide * values_ref[rows, :].astype(F32)).astype(BF16)
    state_ref[...] = dot(inject_ref[...], scaled_ref[...], ((0,), (0,))).astype(BF16)
    log_ref[...] = dot(total, expander[:heads].astype(F32), precision=EXACT)


def local_kernel(
    dim,
    values_ref,
    gate_ref,
    inject_ref,
    read_ref,
    step_ref,
    rate_ref,
    skip_ref,
    out_ref,
    gain_ref,
    state_ref,
    offset_ref,
    part_ref,
):
    channels = values_ref.shape[1]
    heads = channels // dim

    @pl.when(pl.program_id(0) == 0)
    def _():
        state_ref[...] = jnp.zeros_like(state_ref)
        offset_ref[...] = jnp.zeros_like(offset_ref)

    steps = softplus(step_ref[...])
    logs = steps * rate_ref[...]
    i, j = square(BLOCK)
    lower = jnp.where(i >= j, 1.0, 0.0)
    running = dot(logs, lower, ((1,), (1,)), EXACT)
    running_t = dot(lower, logs, ((1,), (1,)), EXACT)
    after = dot(jnp.where(j > i, 1.0, 0.0), logs, ((1,), (1,)), EXACT)
    turned = dot(jnp.where(i == j, 1.0, 0.0), steps, ((1,), (1,)), EXACT)
    expander = expander_of(heads, dim)
    inject = inject_ref[...]
    readout = read_ref[...]
    scores = jnp.where(i >= j, dot(readout, inject, ((1,), (1,))), 0.0)
    per = LANES // dim
    lane = lax.broadcasted_iota(jnp.int32, (BLOCK, LANES), 1)
    for k in range(heads // per):
        cols = slice(k * LANES, (k + 1) * LANES)
        pair = values_ref[:, cols]
        mixes, parts = [], []
        for q in range(per):
            h = k * per + q
            gap = jnp.minimum(running_t[:, h : h + 1] - running[h : h + 1, :], 0.0)
            mixes.append((scores * jnp.exp(gap) * steps[h : h + 1, :]).astype(BF16))
            parts.append(jnp.where(lane // dim == q, pair, jnp.zeros_like(pair)))
        part_ref[:, cols] = dot(jnp.concatenate(mixes, axis=1), jnp.concatenate(parts, axis=0))
    decay = spread(jnp.exp(running_t), expander)
    values = values_ref[...].astype(F32)
    opened = silu(gate_ref[...].astype(F32))
    total = part_ref[...] + skip_ref[...] * values
    total = total + dot(readout, state_ref[...].astype(BF16)) * decay
    out_ref[...] = (total * opened).astype(BF16)
    offset = offset_ref[0:1, :]
    gain_ref[...] = (opened * spread(jnp.exp(running_t + offset), expander)).astype(BF16)
    offset_ref[0:1, :] = offset + running_t[BLOCK - 1 : BLOCK, :]
    scaled = (spread(jnp.exp(after) * turned, expander) * values).astype(BF16)
    state_ref[...] = state_ref[...] * decay[BLOCK - 1 : BLOCK, :] + dot(
        inject, scaled, ((0,), (0,))
    )


def sample_kernel(
    dim,
    length_ref,
    values_ref,
    gate_ref,
    inject_ref,
    read_ref,
    step_ref,
    rate_ref,
    skip_ref,
    out_ref,
    gain_ref,
    picked_ref,
):
    samples, length, channels = values_ref.shape
    heads = channels // dim
    out_ref[...] = jnp.zeros_like(out_ref)
    gain_ref[...] = jnp.zeros_like(gain_ref)
    picked_ref[...] = jnp.zeros_like(picked_ref)
    u, s = square(length)
    own = lax.broadcasted_iota(jnp.int32, (heads, channels), 1) // dim == (
        lax.broadcasted_iota(jnp.int32, (heads, channels), 0)
    )
    at = lax.broadcasted_iota(jnp.int32, (1, length), 1)
    for k in range(samples):
        last = length_ref[k] - 1
        hot = jnp.where(lax.broadcasted_iota(jnp.int32, (PAD, length), 1) == last, 1.0, 0.0).astype(BF16)
        steps = softplus(step_ref[k])
        logs = steps * rate_ref[...]
        between = jnp.where((u > s) & (u <= last), 1.0, 0.0)
        gap = dot(logs, between, precision=EXACT)
        running = jnp.sum(jnp.where(at <= last, logs, 0.0), axis=1, keepdims=True)
        row = dot(hot, read_ref[k])
        score = dot(row.astype(BF16), inject_ref[k], ((1,), (1,)))[0:1]
        mixing = jnp.where(at <= last, score * jnp.exp(gap) * steps, 0.0).astype(BF16)
        values = values_ref[k]
        local = jnp.sum(jnp.where(own, dot(mixing, values), 0.0), axis=0, keepdims=True)
        decay = jnp.sum(jnp.where(own, jnp.exp(running), 0.0), axis=0, keepdims=True)
        value = dot(hot, values)[0:1]
        opened = silu(dot(hot, gate_ref[k])[0:1])
        out_ref[k : k + 1, :] = (local + skip_ref[...] * value) * opened
        gain_ref[k : k + 1, :] = decay * opened
        picked_ref[k : k + 1, :] = row[0:1]


def finish_rows(total, weight):
    mean = jnp.mean(total * total, axis=1, keepdims=True)
    return (total * lax.rsqrt(mean + 1e-05) * weight).astype(BF16)


def finish_kernel(
    read_ref,
    state_ref,
    out_ref,
    gain_ref,
    picked_ref,
    final_ref,
    sample_out_ref,
    sample_gain_ref,
    weight_ref,
    normed_ref,
):
    tokens = read_ref.shape[0]
    for b in range(tokens // BLOCK):
        rows = pl.ds(b * BLOCK, BLOCK)
        arrival = dot(read_ref[rows, :], state_ref[...])
        total = out_ref[rows, :].astype(F32) + arrival * gain_ref[rows, :].astype(F32)
        normed_ref[rows, :] = finish_rows(total, weight_ref[...])
    arrival = dot(picked_ref[...].astype(BF16), final_ref[...])
    total = sample_out_ref[...] + arrival * sample_gain_ref[...]
    normed_ref[pl.ds(tokens, total.shape[0]), :] = finish_rows(total, weight_ref[...])


def scan_states(state, logs, axis):
    peers, place = (lax.axis_size(axis), lax.axis_index(axis))

    def swap(value, stride):
        return lax.ppermute(value, axis, [(p, p ^ stride) for p in range(peers)])

    def join(first, second, second_logs):
        return jnp.exp(second_logs) * first.astype(F32) + second.astype(F32)

    odd = place % 2 == 1
    other, other_logs = swap(state, 1), swap(logs, 1)
    half = state.shape[0] // 2

    def own_half(value):
        return lax.dynamic_slice_in_dim(value, (place % 2) * half, half, 0)

    mine, theirs = own_half(state), own_half(other)
    total = join(
        jnp.where(odd, theirs, mine), jnp.where(odd, mine, theirs), jnp.where(odd, logs, other_logs)
    ).astype(BF16)
    total_logs = logs + other_logs
    before, before_logs = jnp.zeros(total.shape, F32), jnp.zeros_like(logs)
    stride = 2
    while stride < peers:
        upper = (place // stride) % 2 == 1
        far, far_logs = swap(total, stride), swap(total_logs, stride)
        before = jnp.where(upper, join(far, before, before_logs), before)
        before_logs = jnp.where(upper, before_logs + far_logs, before_logs)
        total = join(
            jnp.where(upper, far, total),
            jnp.where(upper, total, far),
            jnp.where(upper, total_logs, far_logs),
        ).astype(BF16)
        total_logs = total_logs + far_logs
        stride *= 2
    pack = jnp.stack([before.astype(BF16), total])
    swapped = swap(pack, 1)
    low, high = jnp.where(odd, swapped, pack), jnp.where(odd, pack, swapped)
    both = jnp.concatenate([low, high], axis=1)
    entered = jnp.where(odd, join(both[0], other, other_logs), both[0].astype(F32))
    return entered.astype(BF16), both[1]


def call(body, outs, scratch=(), flops=0, **more):
    return pl.pallas_call(
        body,
        out_shape=outs,
        scratch_shapes=list(scratch),
        compiler_params=pltpu.CompilerParams(vmem_limit_bytes=VMEM_LIMIT),
        cost_estimate=pl.CostEstimate(flops=flops, bytes_accessed=8 << 20, transcendentals=0),
        **more,
    )


def per_device(
    prompt_values,
    prompt_gate,
    prompt_inject,
    prompt_read,
    prompt_step,
    decay_log,
    skip_gain,
    norm_weight,
    out_weight,
    sample_values,
    sample_gate,
    sample_inject,
    sample_read,
    sample_step,
    sample_length,
):
    tokens, channels = prompt_values.shape
    heads = prompt_step.shape[0]
    dim = channels // heads
    entries = prompt_inject.shape[2]
    samples, length = sample_values.shape[:2]
    inject = prompt_inject.reshape(tokens, entries)
    readout = prompt_read.reshape(tokens, entries)
    rate = -jnp.exp(decay_log)[:, None]
    skip = jnp.repeat(skip_gain, dim)[None]
    weight = norm_weight[None]
    shape = jax.ShapeDtypeStruct

    state, logs = call(
        functools.partial(state_kernel, dim),
        (shape((entries, channels), BF16), shape((PAD, channels), F32)),
        [pltpu.VMEM((tokens, channels), BF16)],
        flops=2 << 30,
    )(prompt_values, inject, prompt_step, rate)

    def block(width):
        return pl.BlockSpec((BLOCK, width), lambda b: (b, 0))

    def whole(*sizes):
        return pl.BlockSpec(sizes, lambda b: (0,) * len(sizes))

    out, gain = call(
        functools.partial(local_kernel, dim),
        (shape((tokens, channels), BF16), shape((tokens, channels), BF16)),
        [
            pltpu.VMEM((entries, channels), F32),
            pltpu.VMEM((PAD, heads), F32),
            pltpu.VMEM((BLOCK, channels), F32),
        ],
        flops=8 << 30,
        grid=(tokens // BLOCK,),
        in_specs=[
            block(channels),
            block(channels),
            block(entries),
            block(entries),
            pl.BlockSpec((heads, BLOCK), lambda b: (0, b)),
            whole(heads, 1),
            whole(1, channels),
        ],
        out_specs=(block(channels), block(channels)),
    )(prompt_values, prompt_gate, inject, readout, prompt_step, rate, skip)
    padded = -(-samples // (2 * PAD)) * 2 * PAD
    vmem = pl.BlockSpec(memory_space=pltpu.VMEM)
    sample_out, sample_gain, picked = call(
        functools.partial(sample_kernel, dim),
        (
            shape((padded, channels), F32),
            shape((padded, channels), F32),
            shape((padded, entries), F32),
        ),
        flops=4 << 30,
        in_specs=[pl.BlockSpec(memory_space=pltpu.SMEM)] + [vmem] * 7,
    )(
        sample_length,
        sample_values,
        sample_gate,
        sample_inject.reshape(samples, length, entries),
        sample_read.reshape(samples, length, entries),
        sample_step.transpose(1, 0, 2),
        rate,
        skip,
    )
    before, final = scan_states(state, logs[:1], "ctx")
    normed = call(finish_kernel, shape((tokens + padded, channels), BF16), flops=1 << 30)(
        readout, before, out, gain, picked, final, sample_out, sample_gain, weight
    )
    return project(normed, out_weight, tokens, samples)


def project_kernel(
    n,
    normed_ref,
    weight_ref,
    out_ref,
    tiles,
    sent,
    from_low,
    from_high,
    tile_sems,
    sent_sems,
    low_sems,
    high_sems,
):
    place = lax.axis_index("head")
    chunks, _, width = out_ref.shape

    def tile_copy(d, c):
        start = (d * chunks + c) * width
        if not isinstance(start, int):
            start = pl.multiple_of(start, width)
        return pltpu.make_async_copy(
            weight_ref.at[:, pl.ds(start, width)],
            tiles.at[d, c],
            tile_sems.at[d, c],
        )

    for k in range((n + 1) // 2):
        for c in range(chunks):
            for d in sorted({n - 1 - k, k}, reverse=True):
                tile_copy(d, c).start()

    barrier = pltpu.get_barrier_semaphore()

    def greet(to):
        pl.semaphore_signal(
            barrier, inc=1, device_id={"head": to}, device_id_type=pl.DeviceIdType.MESH
        )

    @pl.when(place > 0)
    def _():
        greet(place - 1)

    @pl.when(place < n - 1)
    def _():
        greet(place + 1)

    inside = (place > 0) & (place < n - 1)

    @pl.when(inside)
    def _():
        pl.semaphore_wait(barrier, 2)

    @pl.when(jnp.logical_not(inside))
    def _():
        pl.semaphore_wait(barrier, 1)

    def hop(d, c, landing, sems, to):
        return pltpu.make_async_remote_copy(
            src_ref=sent.at[d, c],
            dst_ref=landing.at[d, c],
            send_sem=sent_sems.at[d, c],
            recv_sem=sems.at[d, c],
            device_id={"head": to},
            device_id_type=pl.DeviceIdType.MESH,
        )

    def up(d, c):
        return hop(d, c, from_low, low_sems, place + 1)

    def down(d, c):
        return hop(d, c, from_high, high_sems, place - 1)

    def share(d, c):
        tile_copy(d, c).wait()
        return dot(normed_ref[...], tiles[d, c])

    def pass_on(d, c, move, landing, fed):
        sent[d, c] = share(d, c).astype(BF16)

        @pl.when(fed)
        def _():
            move(d, c).wait_recv()
            sent[d, c] = (sent[d, c].astype(F32) + landing[d, c].astype(F32)).astype(BF16)

        move(d, c).start()

    def turn(t, carry):
        k, c = t // chunks, t % chunks

        @pl.when(place < n - 1 - k)
        def _():
            pass_on(n - 1 - k, c, up, from_low, place > 0)

        @pl.when(place > k)
        def _():
            pass_on(k, c, down, from_high, place < n - 1)

        return carry

    lax.fori_loop(0, (n - 1) * chunks, turn, 0)

    def own(c, carry):
        out_ref[c] = share(place, c).astype(BF16)
        return carry

    lax.fori_loop(0, chunks, own, 0)

    def gather(c, carry):
        @pl.when(place < n - 1)
        def _():
            down(place, c).wait_recv()
            out_ref[c] = (out_ref[c].astype(F32) + from_high[place, c].astype(F32)).astype(BF16)

        @pl.when(place > 0)
        def _():
            up(place, c).wait_recv()
            out_ref[c] = (out_ref[c].astype(F32) + from_low[place, c].astype(F32)).astype(BF16)

        return carry

    lax.fori_loop(0, chunks, gather, 0)

    def drain(t, carry):
        d, c = t // chunks, t % chunks

        @pl.when(d > place)
        def _():
            up(d, c).wait_send()

        @pl.when(d < place)
        def _():
            down(d, c).wait_send()

        return carry

    lax.fori_loop(0, n * chunks, drain, 0)


def project(normed, out_weight, tokens, samples):
    n = lax.axis_size("head")
    rows, depth = normed.shape
    width = 2 * LANES
    chunks = out_weight.shape[1] // n // width
    slots = pltpu.VMEM((n, chunks, rows, width), BF16)
    sems = pltpu.SemaphoreType.DMA((n, chunks))
    mixed = pl.pallas_call(
        functools.partial(project_kernel, n),
        out_shape=jax.ShapeDtypeStruct((chunks, rows, width), BF16),
        in_specs=[
            pl.BlockSpec(memory_space=pltpu.VMEM),
            pl.BlockSpec(memory_space=pl.ANY),
        ],
        out_specs=pl.BlockSpec(memory_space=pltpu.VMEM),
        scratch_shapes=[
            pltpu.VMEM((n, chunks, depth, width), BF16),
            slots,
            slots,
            slots,
            sems,
            sems,
            sems,
            sems,
        ],
        compiler_params=pltpu.CompilerParams(
            collective_id=0, has_side_effects=True, vmem_limit_bytes=VMEM_LIMIT
        ),
    )(normed, out_weight)
    mixed = mixed.transpose(0, 2, 1).reshape(chunks * width, rows)
    return mixed[:, :tokens], mixed[:, tokens : tokens + samples]


def solution(mesh):
    in_specs = (
        P("ctx", "head"),
        P("ctx", "head"),
        P("ctx", "head", None),
        P("ctx", "head", None),
        P("head", "ctx"),
        P("head"),
        P("head"),
        P("head"),
        P("head", None),
        P("ctx", None, "head"),
        P("ctx", None, "head"),
        P("ctx", None, "head", None),
        P("ctx", None, "head", None),
        P("head", "ctx", None),
        P("ctx"),
    )
    out_specs = (P("head", "ctx"), P("head", "ctx"))
    return jax.shard_map(
        per_device, mesh=mesh, in_specs=in_specs, out_specs=out_specs, check_vma=False
    )
```

profile of v0, /device:TPU:10, one launch (start us, length us, event | category | flops | bytes accessed | tf_op | source)
XLA Modules:
  0.0 155.8 jit_solution(3913701137022917108)
XLA Ops:
  0.6 0.7 negate_bitcast_fusion
  1.3 0.7 copy.22.rate_ref
  2.0 5.9 %shard_map.158 = (bf16[256,2048]{1,0:T(8,128)(2,1)}, f32[8,2048]{1,0:T(8,128)}) custom-call(bf16[512,2048]{1,0:T(8,128)(2,1)} %values_ref.4, bf16[512,256]{1,0:T(8,128)(2,1)} %bitcast.39, f32[32,512]{1,0:T(8,128)} %step_ref.3, f32[32,1]{1,0:T(8,128)} %copy.22.rate_ref), custom_call_target="tpu_custom_call" | custom-call | flops 2147483648 | bytes 8388608 | tf_op jit(solution)/shard_map/pallas_call | solution.py:288
  7.9 0.0 collective-permute-start.2
  7.9 0.9 slice.16
  8.7 0.5 collective-permute-start
  9.2 1.5 collective-permute-done
  10.7 0.9 slice_add_fusion
  11.6 1.3 add_convert_fusion.2
  12.9 0.6 collective-permute-start.3
  13.5 1.5 collective-permute-start.1
  15.0 12.1 %collective-permute-done.1 = f32[1,2048]{1,0:T(1,128)S(1)} collective-permute-done((f32[1,2048]{1,0:T(1,128)S(1)}, f32[1,2048]{1,0:T(1,128)S(1)}, u32[]{:S(2)}, u32[]{:S(2)}) %collective-permute-start.1) | collective-permute-done | bytes 8224 | tf_op jit(solution)/shard_map/ppermute | solution.py:209
  27.1 0.2 add_convert_fusion.1
  27.4 1.6 %collective-permute-start.4 = (bf16[128,2048]{1,0:T(8,128)(2,1)S(1)}, bf16[128,2048]{1,0:T(8,128)(2,1)S(1)}, u32[]{:S(2)}, u32[]{:S(2)}) collective-permute-start(bf16[128,2048]{1,0:T(8,128)(2,1)S(1)} %add_convert_fusion.1), channel_id=1, source_target_pairs={{0,16},{4,20},{8,24},{12,28},{16,0},{20,4},{24,8},{28,12},{1,17},{... | collective-permute-start | bytes 1572872 | tf_op jit(solution)/shard_map/ppermute | solution.py:209
  29.0 0.5 collective-permute-start.5
  29.5 0.1 broadcast_in_dim.15
  29.5 0.7 broadcast_in_dim_reshape.3.skip_ref
  30.2 0.7 copy.24
  30.9 9.8 %collective-permute-done.5 = f32[1,2048]{1,0:T(1,128)S(1)} collective-permute-done((f32[1,2048]{1,0:T(1,128)S(1)}, f32[1,2048]{1,0:T(1,128)S(1)}, u32[]{:S(2)}, u32[]{:S(2)}) %collective-permute-start.5) | collective-permute-done | bytes 8224 | tf_op jit(solution)/shard_map/ppermute | solution.py:209
  40.8 0.4 fusion.7
  41.2 1.1 pad_maximum_fusion.1
  42.3 2.5 %shard_map.160 = (f32[16,2048]{1,0:T(8,128)}, f32[16,2048]{1,0:T(8,128)}, f32[16,256]{1,0:T(8,128)}) custom-call(s32[2]{0:T(128)} %length_ref.1, bf16[2,16,2048]{2,1,0:T(8,128)(2,1)} %values_ref.5, bf16[2,16,2048]{2,1,0:T(8,128)(2,1)} %gate_ref.3, bf16[2,16,256]{2,1,0:T(8,128)(2,1)} %bitcast.41, bf16[2,16,256]{2,1,0:T(8,128)(2,1)} %bitcast.42, ...), custom_call_target="tpu_custom_call" | custom-call | flops 4294967296 | bytes 8388608 | tf_op jit(solution)/shard_map/pallas_call | solution.py:324
  44.8 12.2 %shard_map.159 = (bf16[512,2048]{1,0:T(8,128)(2,1)}, bf16[512,2048]{1,0:T(8,128)(2,1)}) custom-call(bf16[512,2048]{1,0:T(8,128)(2,1)} %values_ref.4, bf16[512,2048]{1,0:T(8,128)(2,1)} %gate_ref.2, bf16[512,256]{1,0:T(8,128)(2,1)} %bitcast.40, bf16[512,256]{1,0:T(8,128)(2,1)} %bitcast.30, f32[32,512]{1,0:T(8,128)} %step_ref.3, f32[32,1]{1,0:T(8,128)} %copy.22.rate_ref, ...), custom_call_target="tpu_custom_call" | custom-call | flops 8589934592 | bytes 8388608 | tf_op jit(solution)/shard_map/pallas_call | solution.py:301
  57.1 0.1 broadcast_select_fusion
  57.2 1.0 fusion.5.final_ref
  58.3 1.4 fusion.1.state_ref
  59.6 6.3 %shard_map.161.normed_ref = bf16[528,2048]{1,0:T(8,128)(2,1)} custom-call(bf16[512,256]{1,0:T(8,128)(2,1)} %bitcast.31, bf16[256,2048]{1,0:T(8,128)(2,1)} %fusion.1.state_ref, bf16[512,2048]{1,0:T(8,128)(2,1)} %get-tuple-element.11.out_ref, bf16[512,2048]{1,0:T(8,128)(2,1)} %get-tuple-element.12.gain_ref, f32[16,256]{1,0:T(8,128)} %get-tuple-element.13.picked_ref, ...), custom_call_target="tpu_custom_call" | custom-call | flops 1073741824 | bytes 8388608 | tf_op jit(solution)/shard_map/pallas_call | solution.py:344
  65.9 86.5 %shard_map.162 = bf16[4,528,256]{2,1,0:T(8,128)(2,1)} custom-call(bf16[528,2048]{1,0:T(8,128)(2,1)} %shard_map.161.normed_ref, bf16[2048,4096]{1,0:T(8,128)(2,1)} %weight_ref.1), custom_call_target="tpu_custom_call" | custom-call | tf_op jit(solution)/shard_map/pallas_call | solution.py:496
  152.4 1.4 copy.28
  153.8 0.6 slice.24
  154.4 0.1 slice.23
  154.5 1.3 copy.27
  (11 shorter events, 0.1 us)
Async XLA Ops:
  7.9 21.6 %copy-start.1 = (f32[32]{0:T(128)S(1)}, f32[32]{0:T(128)}, u32[]{:S(2)}) copy-start(f32[32]{0:T(128)} %param.21) | copy-start | bytes 388
  7.9 22.4 %copy-start = (f32[32,2,16]{0,2,1:T(8,128)S(1)}, f32[32,2,16]{0,2,1:T(8,128)}, u32[]{:S(2)}) copy-start(f32[32,2,16]{0,2,1:T(8,128)} %param.28) | copy-start | bytes 12292
  7.9 3.8 %collective-permute-start.2 = (bf16[256,2048]{1,0:T(8,128)(2,1)}, bf16[256,2048]{1,0:T(8,128)(2,1)S(1)}, u32[]{:S(2)}, u32[]{:S(2)}) collective-permute-start(bf16[256,2048]{1,0:T(8,128)(2,1)} %get-tuple-element.10), channel_id=1, source_target_pairs={{0,4},{4,0},{8,12},{12,8},{16,20},{20,16},{24,28},{28,24},{1,5},{5... | collective-permute-start | bytes 3145736 | tf_op jit(solution)/shard_map/ppermute | solution.py:209
  8.7 2.0 %collective-permute-start = (f32[1,2048]{1,0:T(1,128)S(1)}, f32[1,2048]{1,0:T(1,128)S(1)}, u32[]{:S(2)}, u32[]{:S(2)}) collective-permute-start(f32[1,2048]{1,0:T(1,128)S(1)} %slice.16), channel_id=1, source_target_pairs={{0,4},{4,0},{8,12},{12,8},{16,20},{20,16},{24,28},{28,24},{1,5},{5... | collective-permute-start | bytes 24584 | tf_op jit(solution)/shard_map/ppermute | solution.py:209
  12.9 14.2 %collective-permute-start.3 = (bf16[128,2048]{1,0:T(8,128)(2,1)S(1)}, bf16[128,2048]{1,0:T(8,128)(2,1)S(1)}, u32[]{:S(2)}, u32[]{:S(2)}) collective-permute-start(bf16[128,2048]{1,0:T(8,128)(2,1)S(1)} %add_convert_fusion.2), channel_id=1, source_target_pairs={{0,8},{4,12},{8,0},{12,4},{16,24},{20,28},{24,16},{28,20},{1,9},{5... | collective-permute-start | bytes 1572872 | tf_op jit(solution)/shard_map/ppermute | solution.py:209
  13.5 13.6 %collective-permute-start.1 = (f32[1,2048]{1,0:T(1,128)S(1)}, f32[1,2048]{1,0:T(1,128)S(1)}, u32[]{:S(2)}, u32[]{:S(2)}) collective-permute-start(f32[1,2048]{1,0:T(1,128)S(1)} %get-tuple-element.24), channel_id=1, source_target_pairs={{0,8},{4,12},{8,0},{12,4},{16,24},{20,28},{24,16},{28,20},{1,9},{5... | collective-permute-start | bytes 24584 | tf_op jit(solution)/shard_map/ppermute | solution.py:209
  27.4 13.4 %collective-permute-start.4 = (bf16[128,2048]{1,0:T(8,128)(2,1)S(1)}, bf16[128,2048]{1,0:T(8,128)(2,1)S(1)}, u32[]{:S(2)}, u32[]{:S(2)}) collective-permute-start(bf16[128,2048]{1,0:T(8,128)(2,1)S(1)} %add_convert_fusion.1), channel_id=1, source_target_pairs={{0,16},{4,20},{8,24},{12,28},{16,0},{20,4},{24,8},{28,12},{1,17},{... | collective-permute-start | bytes 1572872 | tf_op jit(solution)/shard_map/ppermute | solution.py:209
  29.0 11.8 %collective-permute-start.5 = (f32[1,2048]{1,0:T(1,128)S(1)}, f32[1,2048]{1,0:T(1,128)S(1)}, u32[]{:S(2)}, u32[]{:S(2)}) collective-permute-start(f32[1,2048]{1,0:T(1,128)S(1)} %get-tuple-element.26), channel_id=1, source_target_pairs={{0,16},{4,20},{8,24},{12,28},{16,0},{20,4},{24,8},{28,12},{1,17},{... | collective-permute-start | bytes 24584 | tf_op jit(solution)/shard_map/ppermute | solution.py:209
  42.3 14.8 %collective-permute-start.6 = (bf16[2,128,2048]{2,1,0:T(8,128)(2,1)}, bf16[2,128,2048]{2,1,0:T(8,128)(2,1)S(1)}, u32[]{:S(2)}, u32[]{:S(2)}) collective-permute-start(bf16[2,128,2048]{2,1,0:T(8,128)(2,1)} %pad_maximum_fusion.1), channel_id=1, source_target_pairs={{0,4},{4,0},{8,12},{12,8},{16,20},{20,16},{24,28},{28,24},{1,5},{5... | collective-permute-start | bytes 3145736 | tf_op jit(solution)/shard_map/ppermute | solution.py:209
where the time goes:
time: 156 us
  Pallas kernels  113 us (72%)
  waiting for transfers between devices  23.5 us (15%)
  other arithmetic  7.14 us (5%)
  local copies, waits for them, and re-layouts  6.35 us (4%)
  starting transfers between devices  4.67 us (3%)
    pallas_call x1, Pallas kernels, project(): pl.pallas_call(functools.partial(project_kernel, n), out_shape=jax.ShapeD...  86.5 us
    ppermute x7, waiting for transfers between devices, swap(): return lax.ppermute(value, axis, [(p, p ^ stride) for p in range(peers)])  23.5 us
    pallas_call x1, Pallas kernels, per_device(): call(functools.partial(local_kernel, dim), (shape((tokens, channels), BF1...  12.2 us
    pallas_call x1, Pallas kernels, per_device(): call(finish_kernel, shape((tokens + padded, channels), BF16), flops=1 << 30)  6.29 us
    pallas_call x1, Pallas kernels, per_device(): call(functools.partial(state_kernel, dim), (shape((entries, channels), BF...  5.87 us
    ppermute x7, starting transfers between devices, swap(): return lax.ppermute(value, axis, [(p, p ^ stride) for p in range(peers)])  4.67 us
  transfers between devices with their start and end apart: 7, of which 3 were waited for; matrix products, arithmetic and copies ran while one was open for 2% of the time, Pallas kernels for 9%

commit v1 on v0

v1 whole, which is shorter than its diff:
```python
import functools

import jax
import jax.numpy as jnp
from jax import lax
from jax.experimental import pallas as pl
from jax.experimental.pallas import tpu as pltpu
from jax.sharding import PartitionSpec as P

BLOCK = 128
LANES = 128
PAD = 8
F32 = jnp.float32
BF16 = jnp.bfloat16
EXACT = lax.Precision.HIGHEST
VMEM_LIMIT = 60 * 1024 * 1024


def dot(a, b, dims=((1,), (0,)), precision=None):
    return lax.dot_general(a, b, (dims, ((), ())), precision=precision, preferred_element_type=F32)


def softplus(v):
    return jnp.maximum(v, 0.0) + jnp.log1p(jnp.exp(-jnp.abs(v)))


def silu(v):
    return v / (1.0 + jnp.exp(-v))


def spread(w, expander):
    high = w.astype(BF16)
    low = (w - high.astype(F32)).astype(BF16)
    return dot(jnp.concatenate([high, low], axis=1), expander)


def expander_of(heads, dim):
    row = lax.broadcasted_iota(jnp.int32, (2 * heads, heads * dim), 0)
    lane = lax.broadcasted_iota(jnp.int32, (2 * heads, heads * dim), 1)
    head = lane // dim
    return jnp.where((row == head) | (row == head + heads), 1.0, 0.0).astype(BF16)


def square(n):
    return (
        lax.broadcasted_iota(jnp.int32, (n, n), 0),
        lax.broadcasted_iota(jnp.int32, (n, n), 1),
    )


def finish_rows(total, weight):
    mean = jnp.mean(total * total, axis=1, keepdims=True)
    return (total * lax.rsqrt(mean + 1e-05) * weight).astype(BF16)


CHUNK = 4 * LANES


def turn_over(w):
    return jnp.transpose(w, (1, 0))


def layer_kernel(
    dim,
    n,
    peers,
    length_ref,
    values_hbm,
    gate_hbm,
    inject_ref,
    read_ref,
    step_ref,
    decay_ref,
    gain_in_ref,
    norm_ref,
    weight_hbm,
    svalues_ref,
    sgate_ref,
    sinject_ref,
    sread_ref,
    sstep_ref,
    out_hbm,
    sout_ref,
    values_ref,
    gate_ref,
    tiles_ref,
    steps_ref,
    logs_ref,
    wide_ref,
    expander_ref,
    turned_ref,
    skip_ref,
    mine_state,
    pair_state,
    totals,
    arrived,
    before_ref,
    swap_ref,
    enter_ref,
    log_sent,
    log_got,
    pair_scale,
    scale_ref,
    state_ref,
    offset_ref,
    part_ref,
    local_ref,
    gain_ref,
    normed_ref,
    slocal_ref,
    sgain_ref,
    picked_ref,
    picked_got,
    reply_ref,
    reply_got,
    acc_ref,
    own_ref,
    sent,
    landing,
    ssent,
    slanding,
    sown_ref,
    result_ref,
    value_sems,
    gate_sem,
    tile_sems,
    out_sems,
    log_ssems,
    log_rsems,
    pair_ssems,
    pair_rsems,
    scan_ssems,
    scan_rsems,
    swap_ssems,
    swap_rsems,
    small_ssems,
    small_rsems,
    sent_sems,
    land_sems,
    ssent_sems,
    sland_sems,
):
    tokens, channels = values_ref.shape
    heads = step_ref.shape[0]
    entries = inject_ref.shape[1]
    half = entries // 2
    cols = acc_ref.shape[1]
    chunks = channels // CHUNK
    blocks = tokens // BLOCK
    levels = totals.shape[0] - 1
    place = lax.axis_index("head")
    seat = lax.axis_index("ctx")
    side = seat % 2
    odd = side == 1
    own_rows = pl.ds(pl.multiple_of(side * half, half), half)
    other_rows = pl.ds(pl.multiple_of((1 - side) * half, half), half)

    def lanes_of(c):
        return slice(c * CHUNK, (c + 1) * CHUNK)

    def some_lanes(c):
        return pl.ds(pl.multiple_of(c * CHUNK, CHUNK), CHUNK)

    def value_copy(c):
        return pltpu.make_async_copy(
            values_hbm.at[:, lanes_of(c)], values_ref.at[:, lanes_of(c)], value_sems.at[c]
        )

    gate_copy = pltpu.make_async_copy(gate_hbm, gate_ref, gate_sem.at[0])

    def tile_copy(d):
        return pltpu.make_async_copy(
            weight_hbm.at[:, pl.ds(d * cols, cols)], tiles_ref.at[d], tile_sems.at[d]
        )

    for c in range(chunks):
        value_copy(c).start()
    gate_copy.start()
    for k in range((n + 1) // 2):
        for d in sorted({n - 1 - k, k}, reverse=True):
            tile_copy(d).start()

    def digit(s):
        return (seat // (1 << s)) % 2

    def mate(s):
        return seat + (1 << s) - (2 << s) * digit(s)

    barrier = pltpu.get_barrier_semaphore()

    def greet(device):
        pl.semaphore_signal(
            barrier, inc=1, device_id=device, device_id_type=pl.DeviceIdType.MESH
        )

    for s in range(levels + 1):
        greet({"ctx": mate(s)})

    @pl.when(place > 0)
    def _():
        greet({"head": place - 1})

    @pl.when(place < n - 1)
    def _():
        greet({"head": place + 1})

    rows, lanes = square(heads)
    rate_row = -jnp.exp(decay_ref[...])
    rate = jnp.sum(jnp.where(rows == lanes, rate_row, 0.0), axis=1, keepdims=True)
    steps = softplus(step_ref[...])
    logs = steps * rate
    i, j = square(BLOCK)
    expander_ref[...] = expander_of(heads, dim)
    later = jnp.zeros((heads, 1), F32)
    for b in reversed(range(blocks)):
        span = slice(b * BLOCK, (b + 1) * BLOCK)
        steps_ref[b] = steps[:, span]
        logs_ref[b] = logs[:, span]
        after = dot(logs[:, span], jnp.where(i > j, 1.0, 0.0), precision=EXACT) + later
        later = later + jnp.sum(logs[:, span], axis=1, keepdims=True)
        w = turn_over(jnp.exp(after) * steps[:, span])
        high = w.astype(BF16)
        low = (w - high.astype(F32)).astype(BF16)
        wide_ref[span, :] = jnp.concatenate([high, low], axis=1)
    total_logs = jnp.sum(jnp.where(rows == lanes, later, 0.0), axis=0, keepdims=True)
    total_logs = jnp.broadcast_to(total_logs, (PAD, heads))
    turned_ref[...] = turn_over(inject_ref[...].astype(F32)).astype(BF16)
    top = lax.broadcasted_iota(jnp.int32, (PAD, heads), 0) == 0

    inside = (place > 0) & (place < n - 1)

    @pl.when(inside)
    def _():
        pl.semaphore_wait(barrier, levels + 3)

    @pl.when(jnp.logical_not(inside))
    def _():
        pl.semaphore_wait(barrier, levels + 2)

    def remote(src, dst, ssem, rsem, device):
        return pltpu.make_async_remote_copy(
            src_ref=src,
            dst_ref=dst,
            send_sem=ssem,
            recv_sem=rsem,
            device_id=device,
            device_id_type=pl.DeviceIdType.MESH,
        )

    def log_copy(s):
        return remote(
            log_sent.at[s], log_got.at[s], log_ssems.at[s], log_rsems.at[s], {"ctx": mate(s)}
        )

    def pair_copy(c):
        return remote(
            mine_state.at[c, other_rows],
            pair_state.at[c],
            pair_ssems.at[c],
            pair_rsems.at[c],
            {"ctx": mate(0)},
        )

    def scan_copy(s, c):
        return remote(
            totals.at[s - 1, c],
            arrived.at[s - 1, c],
            scan_ssems.at[s - 1, c],
            scan_rsems.at[s - 1, c],
            {"ctx": mate(s)},
        )

    def swap_copy(c, where):
        return remote(
            swap_ref.at[c],
            enter_ref.at[c, where],
            swap_ssems.at[c],
            swap_rsems.at[c],
            {"ctx": mate(0)},
        )

    log_sent[0] = total_logs
    log_copy(0).start()
    before_logs = [jnp.zeros((PAD, heads), F32)]
    group_logs = [total_logs]

    def exchange_logs(s):
        log_copy(s).wait_recv()
        got, own = log_got[s], group_logs[0]
        upper = digit(s) == 1
        above = jnp.where(upper, own, got)
        if s == 0:
            pair = jnp.where(top, above, jnp.where(odd, got, own))
            pair_scale[...] = spread(jnp.exp(pair), expander_ref[...])
        else:
            both = jnp.where(top, above, before_logs[0])
            scale_ref[s - 1] = spread(jnp.exp(both), expander_ref[...])
            before_logs[0] = before_logs[0] + jnp.where(upper, got, 0.0)
        group_logs[0] = own + got
        if s < levels:
            log_sent[s + 1] = group_logs[0]
            log_copy(s + 1).start()

    def state_of(c):
        value_copy(c).wait()
        wide = dot(wide_ref[...], expander_ref[:, lanes_of(c)])
        scaled = (wide * values_ref[:, lanes_of(c)].astype(F32)).astype(BF16)
        mine_state[c] = dot(turned_ref[...], scaled).astype(BF16)
        pair_copy(c).start()

    def pair_up(c):
        pair_copy(c).wait_recv()
        mine = mine_state[c, own_rows].astype(F32)
        theirs = pair_state[c].astype(F32)
        first, second = jnp.where(odd, theirs, mine), jnp.where(odd, mine, theirs)
        totals[0, c] = (first * pair_scale[0:1, lanes_of(c)] + second).astype(BF16)
        scan_copy(1, c).start()

    for c in range(chunks):
        state_of(c)
        if c <= levels:
            exchange_logs(c)
        if c > 0:
            pair_up(c - 1)
    pair_up(chunks - 1)
    for s in range(chunks, levels + 1):
        exchange_logs(s)
    for s in range(levels + 1):
        log_copy(s).wait_send()

    def scan_step(s, c):
        scan_copy(s, c).wait_recv()
        upper = digit(s) == 1
        far = arrived[s - 1, c].astype(F32)
        near = totals[s - 1, c].astype(F32)
        first, second = jnp.where(upper, far, near), jnp.where(upper, near, far)
        total_scale = scale_ref[s - 1, 0:1, some_lanes(c)]
        totals[s, c] = (first * total_scale + second).astype(BF16)
        if s == 1:
            before = jnp.where(upper, far, 0.0)
        else:
            held = before_ref[c]
            before = jnp.where(upper, far * scale_ref[s - 1, 1:2, some_lanes(c)] + held, held)
        if s < levels:
            before_ref[c] = before
            scan_copy(s + 1, c).start()
        else:
            even_state = jnp.where(odd, pair_state[c].astype(F32), mine_state[c, own_rows].astype(F32))
            moved = before * pair_scale[1:2, some_lanes(c)] + even_state
            enter_ref[c, own_rows] = jnp.where(odd, moved, before).astype(BF16)
            swap_ref[c] = jnp.where(odd, before, moved).astype(BF16)
            swap_copy(c, own_rows).start()

    skip_ref[...] = spread(jnp.broadcast_to(gain_in_ref[...], (PAD, heads)), expander_ref[...])

    def sample_local():
        samples, length = svalues_ref.shape[:2]
        slocal_ref[...] = jnp.zeros_like(slocal_ref)
        sgain_ref[...] = jnp.zeros_like(sgain_ref)
        picked_ref[...] = jnp.zeros_like(picked_ref)
        u, s = square(length)
        own = lax.broadcasted_iota(jnp.int32, (heads, channels), 1) // dim == (
            lax.broadcasted_iota(jnp.int32, (heads, channels), 0)
        )
        at = lax.broadcasted_iota(jnp.int32, (1, length), 1)
        for k in range(samples):
            last = length_ref[k] - 1
            hot = jnp.where(
                lax.broadcasted_iota(jnp.int32, (PAD, length), 1) == last, 1.0, 0.0
            ).astype(BF16)
            tall = softplus(sstep_ref[k])
            tall_logs = tall * rate_row
            flip = ((0,), (0,))
            gap = dot(tall_logs, jnp.where((u > s) & (u <= last), 1.0, 0.0), flip, EXACT)
            running = dot(tall_logs, jnp.where(u <= last, 1.0, 0.0), flip, EXACT)[:, 0:1]
            wide_steps = dot(tall, jnp.where(u == s, 1.0, 0.0), flip, EXACT)
            row = dot(hot, sread_ref[k])
            score = dot(row.astype(BF16), sinject_ref[k], ((1,), (1,)))[0:1]
            mixing = jnp.where(at <= last, score * jnp.exp(gap) * wide_steps, 0.0).astype(BF16)
            values = svalues_ref[k]
            local = jnp.sum(jnp.where(own, dot(mixing, values), 0.0), axis=0, keepdims=True)
            decay = jnp.sum(jnp.where(own, jnp.exp(running), 0.0), axis=0, keepdims=True)
            value = dot(hot, values)[0:1]
            opened = silu(dot(hot, sgate_ref[k])[0:1])
            slocal_ref[k : k + 1, :] = (local + skip_ref[0:1, :] * value) * opened
            sgain_ref[k : k + 1, :] = decay * opened
            picked_ref[k : k + 1, :] = row[0:1].astype(BF16)

    state_ref[...] = jnp.zeros_like(state_ref)
    offset_ref[...] = jnp.zeros_like(offset_ref)
    gate_copy.wait()

    def block_local(b):
        span = pl.ds(pl.multiple_of(b * BLOCK, BLOCK), BLOCK)
        steps, logs = steps_ref[b], logs_ref[b]
        i, j = square(BLOCK)
        lower = jnp.where(i >= j, 1.0, 0.0)
        running = dot(logs, lower, ((1,), (1,)), EXACT)
        running_t = turn_over(running)
        after = turn_over(dot(logs, jnp.where(i > j, 1.0, 0.0), precision=EXACT))
        turned = turn_over(steps)
        expander = expander_ref[...]
        inject = inject_ref[span, :]
        readout = read_ref[span, :]
        scores = jnp.where(i >= j, dot(readout, inject, ((1,), (1,))), 0.0)
        per = LANES // dim
        lane = lax.broadcasted_iota(jnp.int32, (BLOCK, LANES), 1)
        for k in range(heads // per):
            cut = slice(k * LANES, (k + 1) * LANES)
            pair = values_ref[span, cut]
            mixes, parts = [], []
            for q in range(per):
                h = k * per + q
                gap = jnp.minimum(running_t[:, h : h + 1] - running[h : h + 1, :], 0.0)
                mixes.append((scores * jnp.exp(gap) * steps[h : h + 1, :]).astype(BF16))
                parts.append(jnp.where(lane // dim == q, pair, jnp.zeros_like(pair)))
            part_ref[:, cut] = dot(jnp.concatenate(mixes, axis=1), jnp.concatenate(parts, axis=0))
        decay = spread(jnp.exp(running_t), expander)
        values = values_ref[span, :].astype(F32)
        opened = silu(gate_ref[span, :].astype(F32))
        total = part_ref[...] + skip_ref[0:1, :] * values
        total = total + dot(readout, state_ref[...].astype(BF16)) * decay
        local_ref[span, :] = (total * opened).astype(BF16)
        offset = offset_ref[0:1, :]
        gain_ref[span, :] = (opened * spread(jnp.exp(running_t + offset), expander)).astype(BF16)
        offset_ref[0:1, :] = offset + running_t[BLOCK - 1 : BLOCK, :]
        scaled = (spread(jnp.exp(after) * turned, expander) * values).astype(BF16)
        state_ref[...] = state_ref[...] * decay[BLOCK - 1 : BLOCK, :] + dot(
            inject, scaled, ((0,), (0,))
        )

    last_round = chunks + 2 * (levels - 1)

    def small_copy(q, src, dst):
        return remote(src, dst, small_ssems.at[q], small_rsems.at[q], {"ctx": mate(0)})

    picked_copy = small_copy(0, picked_ref, picked_got)
    reply_copy = small_copy(1, reply_ref, reply_got)

    def round_of(t, carry):
        @pl.when(t < blocks)
        def _():
            block_local(t)

        @pl.when(t == blocks)
        def _():
            sample_local()
            picked_copy.start()

        for s in range(1, levels + 1):
            c = t - 2 * (s - 1)

            @pl.when((c >= 0) & (c < chunks))
            def _():
                scan_step(s, c)

        return carry

    lax.fori_loop(0, max(last_round, blocks + 1), round_of, 0)
    for c in range(chunks):
        swap_copy(c, other_rows).wait_recv()
    for d in range(n):
        tile_copy(d).wait()

    def share(rows, d):
        return dot(normed_ref[rows, :], tiles_ref[d])

    def hop_up(d, b):
        return remote(
            sent.at[d, b],
            landing.at[d + 1, b],
            sent_sems.at[d, b],
            land_sems.at[d + 1, b],
            {"head": place + 1},
        )

    def hop_down(d, b):
        return remote(
            sent.at[d, b],
            landing.at[d, b],
            sent_sems.at[d, b],
            land_sems.at[d, b],
            {"head": place - 1},
        )

    def shop_up(d):
        return remote(
            ssent.at[d],
            slanding.at[d + 1],
            ssent_sems.at[d],
            sland_sems.at[d + 1],
            {"head": place + 1},
        )

    def shop_down(d):
        return remote(
            ssent.at[d], slanding.at[d], ssent_sems.at[d], sland_sems.at[d], {"head": place - 1}
        )

    def rows_of(b):
        return pl.ds(pl.multiple_of(b * BLOCK, BLOCK), BLOCK)

    def pass_on(d, b, slot, move, fed):
        acc_ref[...] = share(rows_of(b), d)

        @pl.when(fed)
        def _():
            move(d, b).wait_recv()
            acc_ref[...] = acc_ref[...] + landing[slot, b].astype(F32)

        sent[d, b] = acc_ref[...].astype(BF16)
        move(d, b).start()

    def finish_block(b):
        span = rows_of(b)
        readout = read_ref[span, :]
        pieces = []
        for c in range(chunks):
            arrival = dot(readout, enter_ref[c])
            piece = local_ref[span, lanes_of(c)].astype(F32)
            pieces.append(piece + arrival * gain_ref[span, lanes_of(c)].astype(F32))
        normed_ref[span, :] = finish_rows(jnp.concatenate(pieces, axis=1), norm_ref[...])

    def send_turn(k, b):
        up, down = n - 1 - k, k

        @pl.when(place < up)
        def _():
            pass_on(up, b, up + 1, hop_up, place > 0)

        @pl.when(place > down)
        def _():
            pass_on(down, b, down, hop_down, place < n - 1)

    def first_turn(b, carry):
        finish_block(b)
        send_turn(0, b)
        return carry

    lax.fori_loop(0, blocks, first_turn, 0)

    def half_of(ref):
        return jnp.where(odd, ref[:, half:].astype(F32), ref[:, :half].astype(F32)).astype(BF16)

    picked_copy.wait_recv()
    asked, answered = half_of(picked_got), half_of(picked_ref)
    arrivals = []
    for c in range(chunks):
        reply_ref[:, lanes_of(c)] = dot(asked, totals[levels, c])
        arrivals.append(dot(answered, totals[levels, c]))
    reply_copy.start()
    reply_copy.wait_recv()
    arrival = jnp.concatenate(arrivals, axis=1) + reply_got[...]
    padded = slocal_ref.shape[0]
    srows = pl.ds(tokens, padded)
    normed_ref[srows, :] = finish_rows(slocal_ref[...] + arrival * sgain_ref[...], norm_ref[...])

    def spass_on(d, slot, move, fed):
        sown_ref[...] = share(srows, d)

        @pl.when(fed)
        def _():
            move(d).wait_recv()
            sown_ref[...] = sown_ref[...] + slanding[slot].astype(F32)

        ssent[d] = sown_ref[...].astype(BF16)
        move(d).start()

    def sample_turn(k, carry):
        up, down = n - 1 - k, k

        @pl.when(place < up)
        def _():
            spass_on(up, up + 1, shop_up, place > 0)

        @pl.when(place > down)
        def _():
            spass_on(down, down, shop_down, place < n - 1)

        return carry

    lax.fori_loop(0, n - 1, sample_turn, 0)
    sown_ref[...] = share(srows, place)

    def later_turn(t, carry):
        send_turn(t // blocks, t % blocks)
        return carry

    lax.fori_loop(blocks, (n - 1) * blocks, later_turn, 0)

    def own(b, carry):
        own_ref[b] = share(rows_of(b), place)
        return carry

    lax.fori_loop(0, blocks, own, 0)

    @pl.when(place < n - 1)
    def _():
        shop_down(place).wait_recv()
        sown_ref[...] = sown_ref[...] + slanding[place].astype(F32)

    @pl.when(place > 0)
    def _():
        shop_up(place).wait_recv()
        sown_ref[...] = sown_ref[...] + slanding[place + 1].astype(F32)

    sout_ref[...] = sown_ref[...].astype(BF16)

    def out_copy(b):
        return pltpu.make_async_copy(
            result_ref.at[b], out_hbm.at[pl.ds(pl.multiple_of(b * BLOCK, BLOCK), BLOCK)], out_sems.at[b]
        )

    def gather(b, carry):
        @pl.when(place < n - 1)
        def _():
            hop_down(place, b).wait_recv()
            own_ref[b] = own_ref[b] + landing[place, b].astype(F32)

        @pl.when(place > 0)
        def _():
            hop_up(place, b).wait_recv()
            own_ref[b] = own_ref[b] + landing[place + 1, b].astype(F32)

        result_ref[b] = own_ref[b].astype(BF16)
        out_copy(b).start()
        return carry

    lax.fori_loop(0, blocks, gather, 0)

    def drain(t, carry):
        d, b = t // blocks, t % blocks

        @pl.when(d > place)
        def _():
            hop_up(d, b).wait_send()

        @pl.when(d < place)
        def _():
            hop_down(d, b).wait_send()

        return carry

    lax.fori_loop(0, n * blocks, drain, 0)

    def sdrain(d, carry):
        @pl.when(d > place)
        def _():
            shop_up(d).wait_send()

        @pl.when(d < place)
        def _():
            shop_down(d).wait_send()

        return carry

    lax.fori_loop(0, n, sdrain, 0)
    for c in range(chunks):
        pair_copy(c).wait_send()
        swap_copy(c, own_rows).wait_send()
        for s in range(1, levels + 1):
            scan_copy(s, c).wait_send()
    picked_copy.wait_send()
    reply_copy.wait_send()
    for b in range(blocks):
        out_copy(b).wait()


def per_device(
    prompt_values,
    prompt_gate,
    prompt_inject,
    prompt_read,
    prompt_step,
    decay_log,
    skip_gain,
    norm_weight,
    out_weight,
    sample_values,
    sample_gate,
    sample_inject,
    sample_read,
    sample_step,
    sample_length,
):
    n, peers = lax.axis_size("head"), lax.axis_size("ctx")
    levels = peers.bit_length() - 2
    tokens, channels = prompt_values.shape
    heads = prompt_step.shape[0]
    dim = channels // heads
    entries = prompt_inject.shape[2]
    half = entries // 2
    samples, length = sample_values.shape[:2]
    padded = -(-samples // (2 * PAD)) * 2 * PAD
    cols = out_weight.shape[1] // n
    blocks, chunks = tokens // BLOCK, channels // CHUNK
    vmem = pl.BlockSpec(memory_space=pltpu.VMEM)
    hbm = pl.BlockSpec(memory_space=pl.ANY)
    dma = pltpu.SemaphoreType.DMA
    shape = jax.ShapeDtypeStruct
    V = pltpu.VMEM
    mixed, smixed = pl.pallas_call(
        functools.partial(layer_kernel, dim, n, peers),
        out_shape=(shape((tokens, cols), BF16), shape((padded, cols), BF16)),
        in_specs=[
            pl.BlockSpec(memory_space=pltpu.SMEM),
            hbm,
            hbm,
            vmem,
            vmem,
            vmem,
            vmem,
            vmem,
            vmem,
            hbm,
            vmem,
            vmem,
            vmem,
            vmem,
            vmem,
        ],
        out_specs=(hbm, vmem),
        scratch_shapes=[
            V((tokens, channels), BF16),
            V((tokens, channels), BF16),
            V((n, channels, cols), BF16),
            V((blocks, heads, BLOCK), F32),
            V((blocks, heads, BLOCK), F32),
            V((tokens, 2 * heads), BF16),
            V((2 * heads, channels), BF16),
            V((entries, tokens), BF16),
            V((PAD, channels), F32),
            V((chunks, entries, CHUNK), BF16),
            V((chunks, half, CHUNK), BF16),
            V((levels + 1, chunks, half, CHUNK), BF16),
            V((levels, chunks, half, CHUNK), BF16),
            V((chunks, half, CHUNK), F32),
            V((chunks, half, CHUNK), BF16),
            V((chunks, entries, CHUNK), BF16),
            V((levels + 1, PAD, heads), F32),
            V((levels + 1, PAD, heads), F32),
            V((PAD, channels), F32),
            V((levels, PAD, channels), F32),
            V((entries, channels), F32),
            V((PAD, heads), F32),
            V((BLOCK, channels), F32),
            V((tokens, channels), BF16),
            V((tokens, channels), BF16),
            V((tokens + padded, channels), BF16),
            V((padded, channels), F32),
            V((padded, channels), F32),
            V((padded, entries), BF16),
            V((padded, entries), BF16),
            V((padded, channels), F32),
            V((padded, channels), F32),
            V((BLOCK, cols), F32),
            V((blocks, BLOCK, cols), F32),
            V((n, blocks, BLOCK, cols), BF16),
            V((n + 1, blocks, BLOCK, cols), BF16),
            V((n, padded, cols), BF16),
            V((n + 1, padded, cols), BF16),
            V((padded, cols), F32),
            V((blocks, BLOCK, cols), BF16),
            dma((chunks,)),
            dma((1,)),
            dma((n,)),
            dma((blocks,)),
            dma((levels + 1,)),
            dma((levels + 1,)),
            dma((chunks,)),
            dma((chunks,)),
            dma((levels, chunks)),
            dma((levels, chunks)),
            dma((chunks,)),
            dma((chunks,)),
            dma((2,)),
            dma((2,)),
            dma((n, blocks)),
            dma((n + 1, blocks)),
            dma((n,)),
            dma((n + 1,)),
        ],
        compiler_params=pltpu.CompilerParams(
            collective_id=0, has_side_effects=True, vmem_limit_bytes=VMEM_LIMIT
        ),
    )(
        sample_length,
        prompt_values,
        prompt_gate,
        prompt_inject.reshape(tokens, entries),
        prompt_read.reshape(tokens, entries),
        prompt_step,
        decay_log[None],
        skip_gain[None],
        norm_weight[None],
        out_weight,
        sample_values,
        sample_gate,
        sample_inject.reshape(samples, length, entries),
        sample_read.reshape(samples, length, entries),
        sample_step.transpose(1, 2, 0),
    )
    return mixed.T, smixed[:samples].T


def solution(mesh):
    in_specs = (
        P("ctx", "head"),
        P("ctx", "head"),
        P("ctx", "head", None),
        P("ctx", "head", None),
        P("head", "ctx"),
        P("head"),
        P("head"),
        P("head"),
        P("head", None),
        P("ctx", None, "head"),
        P("ctx", None, "head"),
        P("ctx", None, "head", None),
        P("ctx", None, "head", None),
        P("head", "ctx", None),
        P("ctx"),
    )
    out_specs = (P("head", "ctx"), P("head", "ctx"))
    return jax.shard_map(
        per_device, mesh=mesh, in_specs=in_specs, out_specs=out_specs, check_vma=False
    )
```

time: 156 us -> 132 us (0.85)
  the two profiles are of different devices: /device:TPU:10 before, /device:TPU:21 now
where the time goes in v1:
time: 132 us
  Pallas kernels  128 us (97%)
  local copies, waits for them, and re-layouts  3.59 us (3%)
    pallas_call x1, Pallas kernels, per_device(): pl.pallas_call(functools.partial(layer_kernel, dim, n, peers), out_shape=...  128 us

profile of v1, /device:TPU:21, one launch (start us, length us, event | category | flops | bytes accessed | tf_op | source)
XLA Modules:
  0.0 131.8 jit_solution(13169861568267091265)
XLA Ops:
  0.6 127.6 %shard_map.158 = (bf16[512,1024]{1,0:T(8,128)(2,1)}, bf16[16,1024]{1,0:T(8,128)(2,1)}) custom-call(s32[2]{0:T(128)} %length_ref.1, bf16[512,2048]{1,0:T(8,128)(2,1)} %values_hbm.1, bf16[512,2048]{1,0:T(8,128)(2,1)} %gate_hbm.1, bf16[512,256]{1,0:T(8,128)(2,1)} %bitcast.12, bf16[512,256]{1,0:T(8,128)(2,1)} %bitcast.13, f32[32,512]{1,0:T(8,128)} %step_ref.1, ...), custom_call_target="tpu_custom_call" | custom-call | tf_op jit(solution)/shard_map/pallas_call | solution.py:702
  128.2 2.3 %copy.17 = bf16[1024,512]{1,0:T(8,128)(2,1)} copy(bf16[1024,512]{0,1:T(8,128)(2,1)} %bitcast.11) | data formatting | bytes 2097152
  130.5 1.3 slice_bitcast_fusion

commit v2 on v1

--- a/solution.py
+++ b/solution.py
@@ -53,7 +53,8 @@
     return (total * lax.rsqrt(mean + 1e-05) * weight).astype(BF16)
 
 
-CHUNK = 4 * LANES
+CHUNK = 2 * LANES
+LAG = 3
 
 
 def turn_over(w):
@@ -99,6 +100,7 @@
     enter_ref,
     log_sent,
     log_got,
+    before_logs,
     pair_scale,
     scale_ref,
     state_ref,
@@ -228,6 +230,16 @@
     top = lax.broadcasted_iota(jnp.int32, (PAD, heads), 0) == 0
 
     inside = (place > 0) & (place < n - 1)
+    log_sent[0] = total_logs
+    before_logs[...] = jnp.zeros_like(before_logs)
+
+    def state_of(c):
+        value_copy(c).wait()
+        wide = dot(wide_ref[...], expander_ref[:, lanes_of(c)])
+        scaled = (wide * values_ref[:, lanes_of(c)].astype(F32)).astype(BF16)
+        mine_state[c] = dot(turned_ref[...], scaled).astype(BF16)
+
+    state_of(0)
 
     @pl.when(inside)
     def _():
@@ -279,34 +291,23 @@
             {"ctx": mate(0)},
         )
 
-    log_sent[0] = total_logs
     log_copy(0).start()
-    before_logs = [jnp.zeros((PAD, heads), F32)]
-    group_logs = [total_logs]
 
     def exchange_logs(s):
         log_copy(s).wait_recv()
-        got, own = log_got[s], group_logs[0]
+        got, own = log_got[s], log_sent[s]
         upper = digit(s) == 1
         above = jnp.where(upper, own, got)
         if s == 0:
             pair = jnp.where(top, above, jnp.where(odd, got, own))
             pair_scale[...] = spread(jnp.exp(pair), expander_ref[...])
         else:
-            both = jnp.where(top, above, before_logs[0])
-            scale_ref[s - 1] = spread(jnp.exp(both), expander_ref[...])
-            before_logs[0] = before_logs[0] + jnp.where(upper, got, 0.0)
-        group_logs[0] = own + got
+            held = before_logs[...]
+            scale_ref[s - 1] = spread(jnp.exp(jnp.where(top, above, held)), expander_ref[...])
+            before_logs[...] = held + jnp.where(upper, got, 0.0)
         if s < levels:
-            log_sent[s + 1] = group_logs[0]
+            log_sent[s + 1] = own + got
             log_copy(s + 1).start()
-
-    def state_of(c):
-        value_copy(c).wait()
-        wide = dot(wide_ref[...], expander_ref[:, lanes_of(c)])
-        scaled = (wide * values_ref[:, lanes_of(c)].astype(F32)).astype(BF16)
-        mine_state[c] = dot(turned_ref[...], scaled).astype(BF16)
-        pair_copy(c).start()
 
     def pair_up(c):
         pair_copy(c).wait_recv()
@@ -316,17 +317,16 @@
         totals[0, c] = (first * pair_scale[0:1, lanes_of(c)] + second).astype(BF16)
         scan_copy(1, c).start()
 
-    for c in range(chunks):
+    pair_copy(0).start()
+    for c in range(1, chunks):
         state_of(c)
-        if c <= levels:
-            exchange_logs(c)
-        if c > 0:
-            pair_up(c - 1)
-    pair_up(chunks - 1)
-    for s in range(chunks, levels + 1):
-        exchange_logs(s)
-    for s in range(levels + 1):
-        log_copy(s).wait_send()
+        pair_copy(c).start()
+        if c == 2:
+            exchange_logs(0)
+        if c > 2:
+            pair_up(c - 3)
+    for c in range(chunks - 3, chunks):
+        pair_up(c)
 
     def scan_step(s, c):
         scan_copy(s, c).wait_recv()
@@ -390,7 +390,7 @@
     offset_ref[...] = jnp.zeros_like(offset_ref)
     gate_copy.wait()
 
-    def block_local(b):
+    def block_local(b, hook):
         span = pl.ds(pl.multiple_of(b * BLOCK, BLOCK), BLOCK)
         steps, logs = steps_ref[b], logs_ref[b]
         i, j = square(BLOCK)
@@ -415,6 +415,8 @@
                 mixes.append((scores * jnp.exp(gap) * steps[h : h + 1, :]).astype(BF16))
                 parts.append(jnp.where(lane // dim == q, pair, jnp.zeros_like(pair)))
             part_ref[:, cut] = dot(jnp.concatenate(mixes, axis=1), jnp.concatenate(parts, axis=0))
+            if 2 * (k + 1) == heads // per:
+                hook(2 * b)
         decay = spread(jnp.exp(running_t), expander)
         values = values_ref[span, :].astype(F32)
         opened = silu(gate_ref[span, :].astype(F32))
@@ -428,35 +430,40 @@
         state_ref[...] = state_ref[...] * decay[BLOCK - 1 : BLOCK, :] + dot(
             inject, scaled, ((0,), (0,))
         )
-
-    last_round = chunks + 2 * (levels - 1)
-
-    def small_copy(q, src, dst):
-        return remote(src, dst, small_ssems.at[q], small_rsems.at[q], {"ctx": mate(0)})
-
-    picked_copy = small_copy(0, picked_ref, picked_got)
-    reply_copy = small_copy(1, reply_ref, reply_got)
-
-    def round_of(t, carry):
-        @pl.when(t < blocks)
-        def _():
-            block_local(t)
-
-        @pl.when(t == blocks)
-        def _():
-            sample_local()
-            picked_copy.start()
-
+        hook(2 * b + 1)
+
+    def hook(g):
         for s in range(1, levels + 1):
-            c = t - 2 * (s - 1)
+
+            @pl.when(g == s - 1)
+            def _():
+                exchange_logs(s)
+
+        for s in range(1, levels + 1):
+            c = g - LAG * (s - 1)
 
             @pl.when((c >= 0) & (c < chunks))
             def _():
                 scan_step(s, c)
 
+    def small_copy(q, src, dst):
+        return remote(src, dst, small_ssems.at[q], small_rsems.at[q], {"ctx": mate(0)})
+
+    picked_copy = small_copy(0, picked_ref, picked_got)
+    reply_copy = small_copy(1, reply_ref, reply_got)
+
+    def round_of(t, carry):
+        block_local(t, hook)
         return carry
 
-    lax.fori_loop(0, max(last_round, blocks + 1), round_of, 0)
+    def late_round(g, carry):
+        hook(g)
+        return carry
+
+    lax.fori_loop(0, blocks, round_of, 0)
+    sample_local()
+    picked_copy.start()
+    lax.fori_loop(2 * blocks, max(chunks + LAG * (levels - 1), 2 * blocks), late_round, 0)
     for c in range(chunks):
         swap_copy(c, other_rows).wait_recv()
     for d in range(n):
@@ -521,39 +528,26 @@
             pieces.append(piece + arrival * gain_ref[span, lanes_of(c)].astype(F32))
         normed_ref[span, :] = finish_rows(jnp.concatenate(pieces, axis=1), norm_ref[...])
 
-    def send_turn(k, b):
-        up, down = n - 1 - k, k
-
-        @pl.when(place < up)
-        def _():
-            pass_on(up, b, up + 1, hop_up, place > 0)
-
-        @pl.when(place > down)
-        def _():
-            pass_on(down, b, down, hop_down, place < n - 1)
-
-    def first_turn(b, carry):
-        finish_block(b)
-        send_turn(0, b)
-        return carry
-
-    lax.fori_loop(0, blocks, first_turn, 0)
-
     def half_of(ref):
         return jnp.where(odd, ref[:, half:].astype(F32), ref[:, :half].astype(F32)).astype(BF16)
 
-    picked_copy.wait_recv()
-    asked, answered = half_of(picked_got), half_of(picked_ref)
-    arrivals = []
-    for c in range(chunks):
-        reply_ref[:, lanes_of(c)] = dot(asked, totals[levels, c])
-        arrivals.append(dot(answered, totals[levels, c]))
-    reply_copy.start()
-    reply_copy.wait_recv()
-    arrival = jnp.concatenate(arrivals, axis=1) + reply_got[...]
     padded = slocal_ref.shape[0]
     srows = pl.ds(tokens, padded)
-    normed_ref[srows, :] = finish_rows(slocal_ref[...] + arrival * sgain_ref[...], norm_ref[...])
+
+    def answer():
+        picked_copy.wait_recv()
+        asked = half_of(picked_got)
+        for c in range(chunks):
+            reply_ref[:, lanes_of(c)] = dot(asked, totals[levels, c])
+        reply_copy.start()
+
+    def finish_samples():
+        reply_copy.wait_recv()
+        answered = half_of(picked_ref)
+        arrivals = [dot(answered, totals[levels, c]) for c in range(chunks)]
+        arrival = jnp.concatenate(arrivals, axis=1) + reply_got[...]
+        total = slocal_ref[...] + arrival * sgain_ref[...]
+        normed_ref[srows, :] = finish_rows(total, norm_ref[...])
 
     def spass_on(d, slot, move, fed):
         sown_ref[...] = share(srows, d)
@@ -566,27 +560,45 @@
         ssent[d] = sown_ref[...].astype(BF16)
         move(d).start()
 
-    def sample_turn(k, carry):
-        up, down = n - 1 - k, k
-
-        @pl.when(place < up)
-        def _():
-            spass_on(up, up + 1, shop_up, place > 0)
-
-        @pl.when(place > down)
-        def _():
-            spass_on(down, down, shop_down, place < n - 1)
+    def step(t, carry):
+        @pl.when(t < blocks)
+        def _():
+            finish_block(t)
+
+        @pl.when(t == min(1, blocks - 1))
+        def _():
+            answer()
+
+        @pl.when(t == blocks - 1)
+        def _():
+            finish_samples()
+
+        rising, falling = t - place, t - (n - 1 - place)
+        up, down = n - 1 - rising // blocks, falling // blocks
+
+        @pl.when((rising >= 0) & (up > place))
+        def _():
+            pass_on(up, rising % blocks, up + 1, hop_up, place > 0)
+
+        @pl.when((falling >= 0) & (down < place))
+        def _():
+            pass_on(down, falling % blocks, down, hop_down, place < n - 1)
+
+        srising, sfalling = rising - (blocks - 1), falling - (blocks - 1)
+        sup, sdown = n - 1 - srising, sfalling
+
+        @pl.when((srising >= 0) & (sup > place))
+        def _():
+            spass_on(sup, sup + 1, shop_up, place > 0)
+
+        @pl.when((sfalling >= 0) & (sdown < place))
+        def _():
+            spass_on(sdown, sdown, shop_down, place < n - 1)
 
         return carry
 
-    lax.fori_loop(0, n - 1, sample_turn, 0)
+    lax.fori_loop(0, (n - 1) * max(blocks, 2), step, 0)
     sown_ref[...] = share(srows, place)
-
-    def later_turn(t, carry):
-        send_turn(t // blocks, t % blocks)
-        return carry
-
-    lax.fori_loop(blocks, (n - 1) * blocks, later_turn, 0)
 
     def own(b, carry):
         own_ref[b] = share(rows_of(b), place)
@@ -604,11 +616,13 @@
         shop_up(place).wait_recv()
         sown_ref[...] = sown_ref[...] + slanding[place + 1].astype(F32)
 
-    sout_ref[...] = sown_ref[...].astype(BF16)
+    sout_ref[...] = sown_ref[0 : sout_ref.shape[0], :].astype(BF16)
 
     def out_copy(b):
         return pltpu.make_async_copy(
-            result_ref.at[b], out_hbm.at[pl.ds(pl.multiple_of(b * BLOCK, BLOCK), BLOCK)], out_sems.at[b]
+            result_ref.at[b],
+            out_hbm.at[:, pl.ds(pl.multiple_of(b * BLOCK, BLOCK), BLOCK)],
+            out_sems.at[b],
         )
 
     def gather(b, carry):
@@ -622,7 +636,7 @@
             hop_up(place, b).wait_recv()
             own_ref[b] = own_ref[b] + landing[place + 1, b].astype(F32)
 
-        result_ref[b] = own_ref[b].astype(BF16)
+        result_ref[b] = turn_over(own_ref[b]).astype(BF16)
         out_copy(b).start()
         return carry
 
@@ -660,6 +674,8 @@
         swap_copy(c, own_rows).wait_send()
         for s in range(1, levels + 1):
             scan_copy(s, c).wait_send()
+    for s in range(levels + 1):
+        log_copy(s).wait_send()
     picked_copy.wait_send()
     reply_copy.wait_send()
     for b in range(blocks):
@@ -701,7 +717,7 @@
     V = pltpu.VMEM
     mixed, smixed = pl.pallas_call(
         functools.partial(layer_kernel, dim, n, peers),
-        out_shape=(shape((tokens, cols), BF16), shape((padded, cols), BF16)),
+        out_shape=(shape((cols, tokens), BF16), shape((samples, cols), BF16)),
         in_specs=[
             pl.BlockSpec(memory_space=pltpu.SMEM),
             hbm,
@@ -739,6 +755,7 @@
             V((chunks, entries, CHUNK), BF16),
             V((levels + 1, PAD, heads), F32),
             V((levels + 1, PAD, heads), F32),
+            V((PAD, heads), F32),
             V((PAD, channels), F32),
             V((levels, PAD, channels), F32),
             V((entries, channels), F32),
@@ -760,7 +777,7 @@
             V((n, padded, cols), BF16),
             V((n + 1, padded, cols), BF16),
             V((padded, cols), F32),
-            V((blocks, BLOCK, cols), BF16),
+            V((blocks, cols, BLOCK), BF16),
             dma((chunks,)),
             dma((1,)),
             dma((n,)),
@@ -800,7 +817,7 @@
         sample_read.reshape(samples, length, entries),
         sample_step.transpose(1, 2, 0),
     )
-    return mixed.T, smixed[:samples].T
+    return mixed, smixed.T
 
 
 def solution(mesh):

time: 132 us -> 105 us (0.80)
  Pallas kernels: 128 us -> 102 us
    pallas_call x1, Pallas kernels: 128 us -> 102 us  [per_device(): pl.pallas_call(functools.partial(layer_kernel, dim, n, peers), out_shape=...]
    unnamed x1 -> x4, local copies, waits for them, and re-layouts: 2.28 us -> 2.86 us
where the time goes in v2:
time: 105 us
  Pallas kernels  102 us (97%)
  local copies, waits for them, and re-layouts  2.86 us (3%)
    pallas_call x1, Pallas kernels, per_device(): pl.pallas_call(functools.partial(layer_kernel, dim, n, peers), out_shape=...  102 us
    unnamed x4, local copies, waits for them, and re-layouts  2.86 us

profile of v2, /device:TPU:21, one launch (start us, length us, event | category | flops | bytes accessed | tf_op | source)
XLA Modules:
  0.0 105.1 jit_solution(6328425877206276050)
XLA Ops:
  0.6 101.5 %shard_map.158 = (bf16[1024,512]{1,0:T(8,128)(2,1)}, bf16[2,1024]{1,0:T(2,128)(2,1)}) custom-call(s32[2]{0:T(128)} %length_ref.1, bf16[512,2048]{1,0:T(8,128)(2,1)} %values_hbm.1, bf16[512,2048]{1,0:T(8,128)(2,1)} %gate_hbm.1, bf16[512,256]{1,0:T(8,128)(2,1)} %bitcast.9, bf16[512,256]{1,0:T(8,128)(2,1)} %bitcast.10, f32[32,512]{1,0:T(8,128)} %step_ref.1, ...), custom_call_target="tpu_custom_call" | custom-call | tf_op jit(solution)/shard_map/pallas_call | solution.py:718
  102.2 0.0 copy-start
  102.2 2.3 %copy.19 = bf16[1024,512]{1,0:T(8,128)(2,1)} copy(bf16[1024,512]{1,0:T(8,128)(2,1)} %get-tuple-element.8) | data formatting | bytes 2097152
  104.5 0.0 copy-done
  104.5 0.6 copy.20
Async XLA Ops:
  102.2 2.3 %copy-start = (bf16[2,1024]{1,0:T(2,128)(2,1)S(1)}, bf16[2,1024]{1,0:T(2,128)(2,1)}, u32[]{:S(2)}) copy-start(bf16[2,1024]{1,0:T(2,128)(2,1)} %get-tuple-element.5) | copy-start | bytes 12292

commit v3 on v2

--- a/solution.py
+++ b/solution.py
@@ -55,6 +55,7 @@
 
 CHUNK = 2 * LANES
 LAG = 3
+EARLY = 2
 
 
 def turn_over(w):
@@ -81,7 +82,7 @@
     sread_ref,
     sstep_ref,
     out_hbm,
-    sout_ref,
+    sout_hbm,
     values_ref,
     gate_ref,
     tiles_ref,
@@ -123,6 +124,7 @@
     slanding,
     sown_ref,
     result_ref,
+    sresult_ref,
     value_sems,
     gate_sem,
     tile_sems,
@@ -178,9 +180,6 @@
     for c in range(chunks):
         value_copy(c).start()
     gate_copy.start()
-    for k in range((n + 1) // 2):
-        for d in sorted({n - 1 - k, k}, reverse=True):
-            tile_copy(d).start()
 
     def digit(s):
         return (seat // (1 << s)) % 2
@@ -212,7 +211,11 @@
     steps = softplus(step_ref[...])
     logs = steps * rate
     i, j = square(BLOCK)
-    expander_ref[...] = expander_of(heads, dim)
+
+    def fill_expander():
+        expander_ref[...] = expander_of(heads, dim)
+
+    fill_expander()
     later = jnp.zeros((heads, 1), F32)
     for b in reversed(range(blocks)):
         span = slice(b * BLOCK, (b + 1) * BLOCK)
@@ -226,7 +229,11 @@
         wide_ref[span, :] = jnp.concatenate([high, low], axis=1)
     total_logs = jnp.sum(jnp.where(rows == lanes, later, 0.0), axis=0, keepdims=True)
     total_logs = jnp.broadcast_to(total_logs, (PAD, heads))
-    turned_ref[...] = turn_over(inject_ref[...].astype(F32)).astype(BF16)
+
+    def turn_inject():
+        turned_ref[...] = turn_over(inject_ref[...].astype(F32)).astype(BF16)
+
+    turn_inject()
     top = lax.broadcasted_iota(jnp.int32, (PAD, heads), 0) == 0
 
     inside = (place > 0) & (place < n - 1)
@@ -326,6 +333,8 @@
         if c > 2:
             pair_up(c - 3)
     for c in range(chunks - 3, chunks):
+        if c == chunks - 1:
+            exchange_logs(1)
         pair_up(c)
 
     def scan_step(s, c):
@@ -389,6 +398,9 @@
     state_ref[...] = jnp.zeros_like(state_ref)
     offset_ref[...] = jnp.zeros_like(offset_ref)
     gate_copy.wait()
+    for k in range((n + 1) // 2):
+        for d in sorted({n - 1 - k, k}, reverse=True):
+            tile_copy(d).start()
 
     def block_local(b, hook):
         span = pl.ds(pl.multiple_of(b * BLOCK, BLOCK), BLOCK)
@@ -415,7 +427,7 @@
                 mixes.append((scores * jnp.exp(gap) * steps[h : h + 1, :]).astype(BF16))
                 parts.append(jnp.where(lane // dim == q, pair, jnp.zeros_like(pair)))
             part_ref[:, cut] = dot(jnp.concatenate(mixes, axis=1), jnp.concatenate(parts, axis=0))
-            if 2 * (k + 1) == heads // per:
+            if hook is not None and 2 * (k + 1) == heads // per:
                 hook(2 * b)
         decay = spread(jnp.exp(running_t), expander)
         values = values_ref[span, :].astype(F32)
@@ -430,10 +442,11 @@
         state_ref[...] = state_ref[...] * decay[BLOCK - 1 : BLOCK, :] + dot(
             inject, scaled, ((0,), (0,))
         )
-        hook(2 * b + 1)
+        if hook is not None:
+            hook(2 * b + 1)
 
     def hook(g):
-        for s in range(1, levels + 1):
+        for s in range(2, levels + 1):
 
             @pl.when(g == s - 1)
             def _():
@@ -460,10 +473,9 @@
         hook(g)
         return carry
 
-    lax.fori_loop(0, blocks, round_of, 0)
-    sample_local()
-    picked_copy.start()
-    lax.fori_loop(2 * blocks, max(chunks + LAG * (levels - 1), 2 * blocks), late_round, 0)
+    early = min(EARLY, blocks)
+    lax.fori_loop(0, early, round_of, 0)
+    lax.fori_loop(2 * early, max(chunks + LAG * (levels - 1), 2 * early), late_round, 0)
     for c in range(chunks):
         swap_copy(c, other_rows).wait_recv()
     for d in range(n):
@@ -549,8 +561,14 @@
         total = slocal_ref[...] + arrival * sgain_ref[...]
         normed_ref[srows, :] = finish_rows(total, norm_ref[...])
 
+    few = sresult_ref.shape[0]
+
+    def sshare(d):
+        wide = share(srows, d)
+        return jnp.concatenate([wide[:few, q * LANES : (q + 1) * LANES] for q in range(cols // LANES)], axis=0)
+
     def spass_on(d, slot, move, fed):
-        sown_ref[...] = share(srows, d)
+        sown_ref[...] = sshare(d)
 
         @pl.when(fed)
         def _():
@@ -565,11 +583,7 @@
         def _():
             finish_block(t)
 
-        @pl.when(t == min(1, blocks - 1))
-        def _():
-            answer()
-
-        @pl.when(t == blocks - 1)
+        @pl.when(t == blocks)
         def _():
             finish_samples()
 
@@ -584,7 +598,7 @@
         def _():
             pass_on(down, falling % blocks, down, hop_down, place < n - 1)
 
-        srising, sfalling = rising - (blocks - 1), falling - (blocks - 1)
+        srising, sfalling = rising - blocks, falling - blocks
         sup, sdown = n - 1 - srising, sfalling
 
         @pl.when((srising >= 0) & (sup > place))
@@ -595,10 +609,23 @@
         def _():
             spass_on(sdown, sdown, shop_down, place < n - 1)
 
+        @pl.when(t + early < blocks)
+        def _():
+            block_local(t + early, None)
+
+        @pl.when(t == blocks - 2)
+        def _():
+            sample_local()
+            picked_copy.start()
+
+        @pl.when(t == blocks - 1)
+        def _():
+            answer()
+
         return carry
 
-    lax.fori_loop(0, (n - 1) * max(blocks, 2), step, 0)
-    sown_ref[...] = share(srows, place)
+    lax.fori_loop(0, (n - 1) * blocks, step, 0)
+    sown_ref[...] = sshare(place)
 
     def own(b, carry):
         own_ref[b] = share(rows_of(b), place)
@@ -616,31 +643,10 @@
         shop_up(place).wait_recv()
         sown_ref[...] = sown_ref[...] + slanding[place + 1].astype(F32)
 
-    sout_ref[...] = sown_ref[0 : sout_ref.shape[0], :].astype(BF16)
-
-    def out_copy(b):
-        return pltpu.make_async_copy(
-            result_ref.at[b],
-            out_hbm.at[:, pl.ds(pl.multiple_of(b * BLOCK, BLOCK), BLOCK)],
-            out_sems.at[b],
-        )
-
-    def gather(b, carry):
-        @pl.when(place < n - 1)
-        def _():
-            hop_down(place, b).wait_recv()
-            own_ref[b] = own_ref[b] + landing[place, b].astype(F32)
-
-        @pl.when(place > 0)
-        def _():
-            hop_up(place, b).wait_recv()
-            own_ref[b] = own_ref[b] + landing[place + 1, b].astype(F32)
-
-        result_ref[b] = turn_over(own_ref[b]).astype(BF16)
-        out_copy(b).start()
-        return carry
-
-    lax.fori_loop(0, blocks, gather, 0)
+    for q in range(cols // LANES):
+        sresult_ref[:, q * LANES : (q + 1) * LANES] = sown_ref[q * few : (q + 1) * few, :].astype(BF16)
+    sout_copy = pltpu.make_async_copy(sresult_ref, sout_hbm, gate_sem.at[1])
+    sout_copy.start()
 
     def drain(t, carry):
         d, b = t // blocks, t % blocks
@@ -678,6 +684,31 @@
         log_copy(s).wait_send()
     picked_copy.wait_send()
     reply_copy.wait_send()
+    def out_copy(b):
+        return pltpu.make_async_copy(
+            result_ref.at[b],
+            out_hbm.at[:, pl.ds(pl.multiple_of(b * BLOCK, BLOCK), BLOCK)],
+            out_sems.at[b],
+        )
+
+    def gather(b, carry):
+        @pl.when(place < n - 1)
+        def _():
+            hop_down(place, b).wait_recv()
+            own_ref[b] = own_ref[b] + landing[place, b].astype(F32)
+
+        @pl.when(place > 0)
+        def _():
+            hop_up(place, b).wait_recv()
+            own_ref[b] = own_ref[b] + landing[place + 1, b].astype(F32)
+
+        result_ref[b] = turn_over(own_ref[b]).astype(BF16)
+        out_copy(b).start()
+        return carry
+
+    lax.fori_loop(0, blocks, gather, 0)
+
+    sout_copy.wait()
     for b in range(blocks):
         out_copy(b).wait()
 
@@ -735,7 +766,7 @@
             vmem,
             vmem,
         ],
-        out_specs=(hbm, vmem),
+        out_specs=(hbm, hbm),
         scratch_shapes=[
             V((tokens, channels), BF16),
             V((tokens, channels), BF16),
@@ -774,12 +805,13 @@
             V((blocks, BLOCK, cols), F32),
             V((n, blocks, BLOCK, cols), BF16),
             V((n + 1, blocks, BLOCK, cols), BF16),
-            V((n, padded, cols), BF16),
-            V((n + 1, padded, cols), BF16),
-            V((padded, cols), F32),
+            V((n, samples * cols // LANES, LANES), BF16),
+            V((n + 1, samples * cols // LANES, LANES), BF16),
+            V((samples * cols // LANES, LANES), F32),
             V((blocks, cols, BLOCK), BF16),
+            V((samples, cols), BF16),
             dma((chunks,)),
-            dma((1,)),
+            dma((2,)),
             dma((n,)),
             dma((blocks,)),
             dma((levels + 1,)),

time: 105 us -> 102 us (0.971); the launches traced: 105 us -> 101 us
  Pallas kernels: 102 us -> 97.2 us
    pallas_call x1, Pallas kernels: 102 us -> 97.2 us  [per_device(): pl.pallas_call(functools.partial(layer_kernel, dim, n, peers), out_shape=...]
where the time goes in v3:
time: 102 us; the launch traced here: 101 us
  Pallas kernels  97.2 us (95%)
  local copies, waits for them, and re-layouts  2.86 us (3%)
    pallas_call x1, Pallas kernels, per_device(): pl.pallas_call(functools.partial(layer_kernel, dim, n, peers), out_shape=...  97.2 us
    unnamed x4, local copies, waits for them, and re-layouts  2.86 us

profile of v3, /device:TPU:21, one launch (start us, length us, event | category | flops | bytes accessed | tf_op | source)
XLA Modules:
  0.0 100.7 jit_solution(18106211027365173062)
XLA Ops:
  0.6 97.2 %shard_map.158 = (bf16[1024,512]{1,0:T(8,128)(2,1)}, bf16[2,1024]{1,0:T(2,128)(2,1)}) custom-call(s32[2]{0:T(128)} %length_ref.1, bf16[512,2048]{1,0:T(8,128)(2,1)} %values_hbm.1, bf16[512,2048]{1,0:T(8,128)(2,1)} %gate_hbm.1, bf16[512,256]{1,0:T(8,128)(2,1)} %bitcast.9, bf16[512,256]{1,0:T(8,128)(2,1)} %bitcast.10, f32[32,512]{1,0:T(8,128)} %step_ref.1, ...), custom_call_target="tpu_custom_call" | custom-call | tf_op jit(solution)/shard_map/pallas_call | solution.py:749
  97.9 0.0 copy-start
  97.9 2.3 %copy.19 = bf16[1024,512]{1,0:T(8,128)(2,1)} copy(bf16[1024,512]{1,0:T(8,128)(2,1)} %get-tuple-element.8) | data formatting | bytes 2097152
  100.1 0.0 copy-done
  100.1 0.6 copy.20
Async XLA Ops:
  97.9 2.3 %copy-start = (bf16[2,1024]{1,0:T(2,128)(2,1)S(1)}, bf16[2,1024]{1,0:T(2,128)(2,1)}, u32[]{:S(2)}) copy-start(bf16[2,1024]{1,0:T(2,128)(2,1)} %get-tuple-element.5) | copy-start | bytes 12292

commit v4 on v3

--- a/solution.py
+++ b/solution.py
@@ -55,7 +55,7 @@
 
 CHUNK = 2 * LANES
 LAG = 3
-EARLY = 2
+HOOKS = 4
 
 
 def turn_over(w):
@@ -70,21 +70,27 @@
     values_hbm,
     gate_hbm,
     inject_ref,
-    read_ref,
+    read_hbm,
     step_ref,
     decay_ref,
     gain_in_ref,
     norm_ref,
     weight_hbm,
+    svalues_hbm,
+    sgate_hbm,
+    sinject_hbm,
+    sread_hbm,
+    sstep_hbm,
+    out_hbm,
+    sout_hbm,
+    values_ref,
+    gate_ref,
+    read_ref,
     svalues_ref,
     sgate_ref,
     sinject_ref,
     sread_ref,
     sstep_ref,
-    out_hbm,
-    sout_hbm,
-    values_ref,
-    gate_ref,
     tiles_ref,
     steps_ref,
     logs_ref,
@@ -107,13 +113,12 @@
     state_ref,
     offset_ref,
     part_ref,
-    local_ref,
     gain_ref,
     normed_ref,
     slocal_ref,
     sgain_ref,
     picked_ref,
-    picked_got,
+    picked_all,
     reply_ref,
     reply_got,
     acc_ref,
@@ -126,7 +131,7 @@
     result_ref,
     sresult_ref,
     value_sems,
-    gate_sem,
+    late_sems,
     tile_sems,
     out_sems,
     log_ssems,
@@ -139,6 +144,8 @@
     swap_rsems,
     small_ssems,
     small_rsems,
+    picked_sems,
+    reply_sems,
     sent_sems,
     land_sems,
     ssent_sems,
@@ -151,7 +158,10 @@
     cols = acc_ref.shape[1]
     chunks = channels // CHUNK
     blocks = tokens // BLOCK
-    levels = totals.shape[0] - 1
+    levels = peers.bit_length() - 2
+    squared = levels == 2
+    log_steps = 2 if squared else levels + 1
+    scan_steps = arrived.shape[0]
     place = lax.axis_index("head")
     seat = lax.axis_index("ctx")
     side = seat % 2
@@ -165,21 +175,30 @@
     def some_lanes(c):
         return pl.ds(pl.multiple_of(c * CHUNK, CHUNK), CHUNK)
 
-    def value_copy(c):
-        return pltpu.make_async_copy(
-            values_hbm.at[:, lanes_of(c)], values_ref.at[:, lanes_of(c)], value_sems.at[c]
-        )
-
-    gate_copy = pltpu.make_async_copy(gate_hbm, gate_ref, gate_sem.at[0])
+    def value_copy(q):
+        lanes = slice(2 * q * CHUNK, 2 * (q + 1) * CHUNK)
+        return pltpu.make_async_copy(values_hbm.at[:, lanes], values_ref.at[:, lanes], value_sems.at[q])
+
+    late = [
+        (gate_hbm, gate_ref),
+        (read_hbm, read_ref),
+        (svalues_hbm, svalues_ref),
+        (sgate_hbm, sgate_ref),
+        (sinject_hbm, sinject_ref),
+        (sread_hbm, sread_ref),
+        (sstep_hbm, sstep_ref),
+    ]
+    late_copies = [pltpu.make_async_copy(*refs, late_sems.at[q]) for q, refs in enumerate(late)]
 
     def tile_copy(d):
         return pltpu.make_async_copy(
             weight_hbm.at[:, pl.ds(d * cols, cols)], tiles_ref.at[d], tile_sems.at[d]
         )
 
-    for c in range(chunks):
-        value_copy(c).start()
-    gate_copy.start()
+    for q in range(chunks // 2):
+        value_copy(q).start()
+    for copy in late_copies:
+        copy.start()
 
     def digit(s):
         return (seat // (1 << s)) % 2
@@ -196,6 +215,18 @@
 
     for s in range(levels + 1):
         greet({"ctx": mate(s)})
+
+    last_seat = peers - 1
+    holds_final = seat == last_seat
+
+    @pl.when(holds_final)
+    def _():
+        for p in range(peers - 1):
+            greet({"ctx": p})
+
+    @pl.when(jnp.logical_not(holds_final))
+    def _():
+        greet({"ctx": last_seat})
 
     @pl.when(place > 0)
     def _():
@@ -240,21 +271,23 @@
     log_sent[0] = total_logs
     before_logs[...] = jnp.zeros_like(before_logs)
 
-    def state_of(c):
-        value_copy(c).wait()
-        wide = dot(wide_ref[...], expander_ref[:, lanes_of(c)])
-        scaled = (wide * values_ref[:, lanes_of(c)].astype(F32)).astype(BF16)
-        mine_state[c] = dot(turned_ref[...], scaled).astype(BF16)
+    def state_of(q):
+        lanes = slice(2 * q * CHUNK, 2 * (q + 1) * CHUNK)
+        value_copy(q).wait()
+        wide = dot(wide_ref[...], expander_ref[:, lanes])
+        scaled = (wide * values_ref[:, lanes].astype(F32)).astype(BF16)
+        state = dot(turned_ref[...], scaled).astype(BF16)
+        mine_state[2 * q] = state[:, :CHUNK]
+        mine_state[2 * q + 1] = state[:, CHUNK:]
 
     state_of(0)
 
-    @pl.when(inside)
-    def _():
-        pl.semaphore_wait(barrier, levels + 3)
-
-    @pl.when(jnp.logical_not(inside))
-    def _():
-        pl.semaphore_wait(barrier, levels + 2)
+    for middle in (False, True):
+        for final in (False, True):
+
+            @pl.when((inside == middle) & (holds_final == final))
+            def _():
+                pl.semaphore_wait(barrier, levels + 2 + middle + (peers - 1 if final else 1))
 
     def remote(src, dst, ssem, rsem, device):
         return pltpu.make_async_remote_copy(
@@ -286,7 +319,7 @@
             arrived.at[s - 1, c],
             scan_ssems.at[s - 1, c],
             scan_rsems.at[s - 1, c],
-            {"ctx": mate(s)},
+            {"ctx": mate(1 if squared and s == 3 else s)},
         )
 
     def swap_copy(c, where):
@@ -310,11 +343,28 @@
             pair_scale[...] = spread(jnp.exp(pair), expander_ref[...])
         else:
             held = before_logs[...]
-            scale_ref[s - 1] = spread(jnp.exp(jnp.where(top, above, held)), expander_ref[...])
+            crossed = jnp.where(digit(2) == 1, jnp.where(upper, got, own), above) if squared else above
+            scale_ref[s - 1] = spread(jnp.exp(jnp.where(top, crossed, held)), expander_ref[...])
             before_logs[...] = held + jnp.where(upper, got, 0.0)
-        if s < levels:
+        if s < log_steps - 1:
             log_sent[s + 1] = own + got
             log_copy(s + 1).start()
+
+    column, row = digit(1), digit(2)
+
+    def at_once(c):
+        if not squared:
+            return seat >= 0
+        if c % 2:
+            return column == 0
+        return (column == 1) & (row == 0)
+
+    def sends(s, c):
+        if not squared:
+            return seat >= 0
+        if s == 1:
+            return column == 0 if c % 2 else row == 0
+        return (column == c % 2) & (row == s - 2)
 
     def pair_up(c):
         pair_copy(c).wait_recv()
@@ -322,20 +372,92 @@
         theirs = pair_state[c].astype(F32)
         first, second = jnp.where(odd, theirs, mine), jnp.where(odd, mine, theirs)
         totals[0, c] = (first * pair_scale[0:1, lanes_of(c)] + second).astype(BF16)
-        scan_copy(1, c).start()
-
-    pair_copy(0).start()
-    for c in range(1, chunks):
-        state_of(c)
-        pair_copy(c).start()
-        if c == 2:
+
+        @pl.when(at_once(c))
+        def _():
+            scan_copy(1, c).start()
+
+    pairs = chunks // 2
+    for q in range(pairs):
+        if q:
+            state_of(q)
+        pair_copy(2 * q + 1).start()
+        pair_copy(2 * q).start()
+        if q == 1:
             exchange_logs(0)
-        if c > 2:
-            pair_up(c - 3)
-    for c in range(chunks - 3, chunks):
-        if c == chunks - 1:
-            exchange_logs(1)
-        pair_up(c)
+        if q > 1:
+            pair_up(2 * q - 3)
+            pair_up(2 * q - 4)
+    for q in range(pairs - 2, pairs):
+        pair_up(2 * q + 1)
+        pair_up(2 * q)
+    if squared:
+        for c in range(0, chunks, 2):
+
+            @pl.when((column == 0) & (row == 0))
+            def _():
+                scan_copy(1, c).start()
+
+    def enter(c, before):
+        even_state = jnp.where(odd, pair_state[c].astype(F32), mine_state[c, own_rows].astype(F32))
+        moved = before * pair_scale[1:2, some_lanes(c)] + even_state
+        enter_ref[c, own_rows] = jnp.where(odd, moved, before).astype(BF16)
+        swap_ref[c] = jnp.where(odd, before, moved).astype(BF16)
+        swap_copy(c, own_rows).start()
+
+    def cross_row(q):
+        c = 2 * q + column
+        scan_copy(1, c).wait_recv()
+        far, near = arrived[0, c].astype(F32), totals[0, c].astype(F32)
+        right = column == 1
+        first, second = jnp.where(right, far, near), jnp.where(right, near, far)
+        totals[1, c] = (first * scale_ref[0, 0:1, some_lanes(c)] + second).astype(BF16)
+        scan_copy(2, c).start()
+        enter(c, jnp.where(right, far, 0.0))
+
+        @pl.when(column == 0)
+        def _():
+            enter(c + 1, jnp.zeros((half, CHUNK), F32))
+
+    def end_row(q):
+        @pl.when(column == 1)
+        def _():
+            scan_copy(1, 2 * q).wait_recv()
+            enter(2 * q, arrived[0, 2 * q].astype(F32))
+
+    def next_row(q):
+        c = 2 * q + column
+        right = column == 1
+
+        @pl.when(right)
+        def _():
+            scan_copy(1, c).wait_recv()
+            totals[0, c] = arrived[0, c]
+
+        scan_copy(2, c).wait_recv()
+        far = arrived[1, c].astype(F32)
+        joined = far * scale_ref[0, 0:1, some_lanes(c)] + totals[0, c].astype(F32)
+        totals[2, c] = jnp.where(right, far, joined).astype(BF16)
+        scan_copy(3, c).start()
+        enter(c, jnp.where(right, joined, far))
+
+    def last_column(q):
+        c = 2 * q + 1 - column
+        scan_copy(3, c).wait_recv()
+        enter(c, arrived[2, c].astype(F32))
+
+    def square_events():
+        first = [(q, cross_row, q) for q in range(pairs)]
+        first += [(q + pairs, end_row, q) for q in range(pairs)]
+        second = [(q, next_row, q) for q in range(pairs)]
+        second += [(q + 2.5, last_column, q) for q in range(pairs)]
+        return [sorted(events, key=lambda event: event[0]) for events in (first, second)]
+
+    def run_events(here, events):
+        @pl.when(here)
+        def _():
+            for _, work, q in events:
+                work(q)
 
     def scan_step(s, c):
         scan_copy(s, c).wait_recv()
@@ -354,11 +476,9 @@
             before_ref[c] = before
             scan_copy(s + 1, c).start()
         else:
-            even_state = jnp.where(odd, pair_state[c].astype(F32), mine_state[c, own_rows].astype(F32))
-            moved = before * pair_scale[1:2, some_lanes(c)] + even_state
-            enter_ref[c, own_rows] = jnp.where(odd, moved, before).astype(BF16)
-            swap_ref[c] = jnp.where(odd, before, moved).astype(BF16)
-            swap_copy(c, own_rows).start()
+            enter(c, before)
+
+    exchange_logs(1)
 
     skip_ref[...] = spread(jnp.broadcast_to(gain_in_ref[...], (PAD, heads)), expander_ref[...])
 
@@ -397,7 +517,8 @@
 
     state_ref[...] = jnp.zeros_like(state_ref)
     offset_ref[...] = jnp.zeros_like(offset_ref)
-    gate_copy.wait()
+    for copy in late_copies:
+        copy.wait()
     for k in range((n + 1) // 2):
         for d in sorted({n - 1 - k, k}, reverse=True):
             tile_copy(d).start()
@@ -428,13 +549,17 @@
                 parts.append(jnp.where(lane // dim == q, pair, jnp.zeros_like(pair)))
             part_ref[:, cut] = dot(jnp.concatenate(mixes, axis=1), jnp.concatenate(parts, axis=0))
             if hook is not None and 2 * (k + 1) == heads // per:
-                hook(2 * b)
+                hook(HOOKS * b)
+        if hook is not None:
+            hook(HOOKS * b + 1)
         decay = spread(jnp.exp(running_t), expander)
         values = values_ref[span, :].astype(F32)
         opened = silu(gate_ref[span, :].astype(F32))
         total = part_ref[...] + skip_ref[0:1, :] * values
         total = total + dot(readout, state_ref[...].astype(BF16)) * decay
-        local_ref[span, :] = (total * opened).astype(BF16)
+        normed_ref[span, :] = (total * opened).astype(BF16)
+        if hook is not None:
+            hook(HOOKS * b + 2)
         offset = offset_ref[0:1, :]
         gain_ref[span, :] = (opened * spread(jnp.exp(running_t + offset), expander)).astype(BF16)
         offset_ref[0:1, :] = offset + running_t[BLOCK - 1 : BLOCK, :]
@@ -443,9 +568,14 @@
             inject, scaled, ((0,), (0,))
         )
         if hook is not None:
-            hook(2 * b + 1)
+            hook(HOOKS * b + 3)
 
     def hook(g):
+        if squared:
+            if g in (0, 1, 3):
+                run_events(row == 0, square_events()[0][g - g // 3 : g - g // 3 + 1])
+            return
+
         for s in range(2, levels + 1):
 
             @pl.when(g == s - 1)
@@ -459,23 +589,27 @@
             def _():
                 scan_step(s, c)
 
-    def small_copy(q, src, dst):
-        return remote(src, dst, small_ssems.at[q], small_rsems.at[q], {"ctx": mate(0)})
-
-    picked_copy = small_copy(0, picked_ref, picked_got)
-    reply_copy = small_copy(1, reply_ref, reply_got)
-
-    def round_of(t, carry):
-        block_local(t, hook)
-        return carry
+    def picked_copy(p):
+        return remote(
+            picked_ref, picked_all.at[p], small_ssems.at[0], picked_sems.at[p], {"ctx": last_seat}
+        )
+
+    def reply_copy(p):
+        return remote(
+            reply_ref.at[p], reply_got, reply_sems.at[p], small_rsems.at[0], {"ctx": p}
+        )
 
     def late_round(g, carry):
         hook(g)
         return carry
 
-    early = min(EARLY, blocks)
-    lax.fori_loop(0, early, round_of, 0)
-    lax.fori_loop(2 * early, max(chunks + LAG * (levels - 1), 2 * early), late_round, 0)
+    block_local(0, hook)
+    if squared:
+        first, second = square_events()
+        run_events(row == 0, first[HOOKS - 1 :])
+        run_events(row == 1, second)
+    else:
+        lax.fori_loop(HOOKS, max(chunks + LAG * (levels - 1), HOOKS), late_round, 0)
     for c in range(chunks):
         swap_copy(c, other_rows).wait_recv()
     for d in range(n):
@@ -536,30 +670,39 @@
         pieces = []
         for c in range(chunks):
             arrival = dot(readout, enter_ref[c])
-            piece = local_ref[span, lanes_of(c)].astype(F32)
+            piece = normed_ref[span, lanes_of(c)].astype(F32)
             pieces.append(piece + arrival * gain_ref[span, lanes_of(c)].astype(F32))
         normed_ref[span, :] = finish_rows(jnp.concatenate(pieces, axis=1), norm_ref[...])
 
-    def half_of(ref):
-        return jnp.where(odd, ref[:, half:].astype(F32), ref[:, :half].astype(F32)).astype(BF16)
-
     padded = slocal_ref.shape[0]
+    few_rows = reply_got.shape[0]
     srows = pl.ds(tokens, padded)
 
     def answer():
-        picked_copy.wait_recv()
-        asked = half_of(picked_got)
+        picked_all[last_seat] = picked_ref[...]
+        for p in range(peers - 1):
+            picked_copy(p).wait_recv()
+        asked = picked_all[...].reshape(peers * padded, entries)
         for c in range(chunks):
-            reply_ref[:, lanes_of(c)] = dot(asked, totals[levels, c])
-        reply_copy.start()
+            final = enter_ref[c].astype(F32) * pair_scale[0:1, lanes_of(c)] + mine_state[c].astype(F32)
+            told = dot(asked, final.astype(BF16))
+            for p in range(peers - 1):
+                reply_ref[p, :, lanes_of(c)] = told[p * padded : p * padded + few_rows]
+            own = told[last_seat * padded : last_seat * padded + few_rows]
+            reply_got[:, lanes_of(c)] = own
+        for p in range(peers - 1):
+            reply_copy(p).start()
 
     def finish_samples():
-        reply_copy.wait_recv()
-        answered = half_of(picked_ref)
-        arrivals = [dot(answered, totals[levels, c]) for c in range(chunks)]
-        arrival = jnp.concatenate(arrivals, axis=1) + reply_got[...]
-        total = slocal_ref[...] + arrival * sgain_ref[...]
-        normed_ref[srows, :] = finish_rows(total, norm_ref[...])
+        @pl.when(jnp.logical_not(holds_final))
+        def _():
+            reply_copy(0).wait_recv()
+
+        total = slocal_ref[:few_rows] + reply_got[...] * sgain_ref[:few_rows]
+        normed = finish_rows(total, norm_ref[...])
+        if few_rows < padded:
+            normed = jnp.concatenate([normed, jnp.zeros((padded - few_rows, channels), BF16)], axis=0)
+        normed_ref[srows, :] = normed
 
     few = sresult_ref.shape[0]
 
@@ -583,7 +726,7 @@
         def _():
             finish_block(t)
 
-        @pl.when(t == blocks)
+        @pl.when(t == blocks + 1)
         def _():
             finish_samples()
 
@@ -598,7 +741,7 @@
         def _():
             pass_on(down, falling % blocks, down, hop_down, place < n - 1)
 
-        srising, sfalling = rising - blocks, falling - blocks
+        srising, sfalling = rising - (blocks + 1), falling - (blocks + 1)
         sup, sdown = n - 1 - srising, sfalling
 
         @pl.when((srising >= 0) & (sup > place))
@@ -609,16 +752,19 @@
         def _():
             spass_on(sdown, sdown, shop_down, place < n - 1)
 
-        @pl.when(t + early < blocks)
-        def _():
-            block_local(t + early, None)
+        @pl.when(t + 1 < blocks)
+        def _():
+            block_local(t + 1, None)
 
         @pl.when(t == blocks - 2)
         def _():
             sample_local()
-            picked_copy.start()
-
-        @pl.when(t == blocks - 1)
+
+            @pl.when(jnp.logical_not(holds_final))
+            def _():
+                picked_copy(seat).start()
+
+        @pl.when((t == blocks - 1) & holds_final)
         def _():
             answer()
 
@@ -645,7 +791,7 @@
 
     for q in range(cols // LANES):
         sresult_ref[:, q * LANES : (q + 1) * LANES] = sown_ref[q * few : (q + 1) * few, :].astype(BF16)
-    sout_copy = pltpu.make_async_copy(sresult_ref, sout_hbm, gate_sem.at[1])
+    sout_copy = pltpu.make_async_copy(sresult_ref, sout_hbm, late_sems.at[len(late)])
     sout_copy.start()
 
     def drain(t, carry):
@@ -678,12 +824,22 @@
     for c in range(chunks):
         pair_copy(c).wait_send()
         swap_copy(c, own_rows).wait_send()
-        for s in range(1, levels + 1):
-            scan_copy(s, c).wait_send()
-    for s in range(levels + 1):
+        for s in range(1, scan_steps + 1):
+
+            @pl.when(sends(s, c))
+            def _():
+                scan_copy(s, c).wait_send()
+    for s in range(log_steps):
         log_copy(s).wait_send()
-    picked_copy.wait_send()
-    reply_copy.wait_send()
+
+    @pl.when(holds_final)
+    def _():
+        for p in range(peers - 1):
+            reply_copy(p).wait_send()
+
+    @pl.when(jnp.logical_not(holds_final))
+    def _():
+        picked_copy(seat).wait_send()
     def out_copy(b):
         return pltpu.make_async_copy(
             result_ref.at[b],
@@ -732,6 +888,7 @@
 ):
     n, peers = lax.axis_size("head"), lax.axis_size("ctx")
     levels = peers.bit_length() - 2
+    scan_steps = 3 if levels == 2 else levels
     tokens, channels = prompt_values.shape
     heads = prompt_step.shape[0]
     dim = channels // heads
@@ -754,22 +911,28 @@
             hbm,
             hbm,
             vmem,
-            vmem,
+            hbm,
             vmem,
             vmem,
             vmem,
             vmem,
             hbm,
-            vmem,
-            vmem,
-            vmem,
-            vmem,
-            vmem,
+            hbm,
+            hbm,
+            hbm,
+            hbm,
+            hbm,
         ],
         out_specs=(hbm, hbm),
         scratch_shapes=[
             V((tokens, channels), BF16),
             V((tokens, channels), BF16),
+            V((tokens, entries), BF16),
+            V(sample_values.shape, BF16),
+            V(sample_gate.shape, BF16),
+            V((samples, length, entries), BF16),
+            V((samples, length, entries), BF16),
+            V((samples, length, heads), F32),
             V((n, channels, cols), BF16),
             V((blocks, heads, BLOCK), F32),
             V((blocks, heads, BLOCK), F32),
@@ -780,7 +943,7 @@
             V((chunks, entries, CHUNK), BF16),
             V((chunks, half, CHUNK), BF16),
             V((levels + 1, chunks, half, CHUNK), BF16),
-            V((levels, chunks, half, CHUNK), BF16),
+            V((scan_steps, chunks, half, CHUNK), BF16),
             V((chunks, half, CHUNK), F32),
             V((chunks, half, CHUNK), BF16),
             V((chunks, entries, CHUNK), BF16),
@@ -793,14 +956,13 @@
             V((PAD, heads), F32),
             V((BLOCK, channels), F32),
             V((tokens, channels), BF16),
-            V((tokens, channels), BF16),
             V((tokens + padded, channels), BF16),
             V((padded, channels), F32),
             V((padded, channels), F32),
             V((padded, entries), BF16),
-            V((padded, entries), BF16),
-            V((padded, channels), F32),
-            V((padded, channels), F32),
+            V((peers, padded, entries), BF16),
+            V((peers - 1, -(-samples // PAD) * PAD, channels), F32),
+            V((-(-samples // PAD) * PAD, channels), F32),
             V((BLOCK, cols), F32),
             V((blocks, BLOCK, cols), F32),
             V((n, blocks, BLOCK, cols), BF16),
@@ -811,19 +973,21 @@
             V((blocks, cols, BLOCK), BF16),
             V((samples, cols), BF16),
             dma((chunks,)),
-            dma((2,)),
+            dma((8,)),
             dma((n,)),
             dma((blocks,)),
             dma((levels + 1,)),
             dma((levels + 1,)),
             dma((chunks,)),
             dma((chunks,)),
-            dma((levels, chunks)),
-            dma((levels, chunks)),
+            dma((scan_steps, chunks)),
+            dma((scan_steps, chunks)),
             dma((chunks,)),
             dma((chunks,)),
-            dma((2,)),
-            dma((2,)),
+            dma((1,)),
+            dma((1,)),
+            dma((peers,)),
+            dma((peers,)),
             dma((n, blocks)),
             dma((n + 1, blocks)),
             dma((n,)),

time: 102 us -> 97.8 us (0.959)
  Pallas kernels: 97.2 us -> 93.9 us
    pallas_call x1, Pallas kernels: 97.2 us -> 93.9 us  [per_device(): pl.pallas_call(functools.partial(layer_kernel, dim, n, peers), out_shape=...]
where the time goes in v4:
time: 97.8 us; the launch traced here: 97.4 us
  Pallas kernels  93.9 us (96%)
  local copies, waits for them, and re-layouts  2.86 us (3%)
    pallas_call x1, Pallas kernels, per_device(): pl.pallas_call(functools.partial(layer_kernel, dim, n, peers), out_shape=...  93.9 us
    unnamed x4, local copies, waits for them, and re-layouts  2.86 us

profile of v4, /device:TPU:21, one launch (start us, length us, event | category | flops | bytes accessed | tf_op | source)
XLA Modules:
  0.0 97.4 jit_solution(10202288486181862174)
XLA Ops:
  0.6 93.9 %shard_map.158 = (bf16[1024,512]{1,0:T(8,128)(2,1)}, bf16[2,1024]{1,0:T(2,128)(2,1)}) custom-call(s32[2]{0:T(128)} %length_ref.1, bf16[512,2048]{1,0:T(8,128)(2,1)} %values_hbm.1, bf16[512,2048]{1,0:T(8,128)(2,1)} %gate_hbm.1, bf16[512,256]{1,0:T(8,128)(2,1)} %bitcast.9, bf16[512,256]{1,0:T(8,128)(2,1)} %bitcast.10, f32[32,512]{1,0:T(8,128)} %step_ref.1, ...), custom_call_target="tpu_custom_call" | custom-call | tf_op jit(solution)/shard_map/pallas_call | solution.py:906
  94.5 0.0 copy-start
  94.6 2.3 %copy.19 = bf16[1024,512]{1,0:T(8,128)(2,1)} copy(bf16[1024,512]{1,0:T(8,128)(2,1)} %get-tuple-element.8) | data formatting | bytes 2097152
  96.8 0.0 copy-done
  96.8 0.6 copy.20
Async XLA Ops:
  94.5 2.3 %copy-start = (bf16[2,1024]{1,0:T(2,128)(2,1)S(1)}, bf16[2,1024]{1,0:T(2,128)(2,1)}, u32[]{:S(2)}) copy-start(bf16[2,1024]{1,0:T(2,128)(2,1)} %get-tuple-element.5) | copy-start | bytes 12292

commit v5 on v4

--- a/solution.py
+++ b/solution.py
@@ -53,7 +53,9 @@
     return (total * lax.rsqrt(mean + 1e-05) * weight).astype(BF16)
 
 
-CHUNK = 2 * LANES
+CHUNK = LANES
+GROUP = 4
+PARTS = 2
 LAG = 3
 HOOKS = 4
 
@@ -113,7 +115,6 @@
     state_ref,
     offset_ref,
     part_ref,
-    gain_ref,
     normed_ref,
     slocal_ref,
     sgain_ref,
@@ -122,7 +123,6 @@
     reply_ref,
     reply_got,
     acc_ref,
-    own_ref,
     sent,
     landing,
     ssent,
@@ -155,7 +155,9 @@
     heads = step_ref.shape[0]
     entries = inject_ref.shape[1]
     half = entries // 2
-    cols = acc_ref.shape[1]
+    cols = weight_hbm.shape[1] // n
+    part = acc_ref.shape[1]
+    per = sent.shape[1]
     chunks = channels // CHUNK
     blocks = tokens // BLOCK
     levels = peers.bit_length() - 2
@@ -175,8 +177,13 @@
     def some_lanes(c):
         return pl.ds(pl.multiple_of(c * CHUNK, CHUNK), CHUNK)
 
+    groups = chunks // GROUP
+
+    def group_lanes(q):
+        return slice(q * GROUP * CHUNK, (q + 1) * GROUP * CHUNK)
+
     def value_copy(q):
-        lanes = slice(2 * q * CHUNK, 2 * (q + 1) * CHUNK)
+        lanes = group_lanes(q)
         return pltpu.make_async_copy(values_hbm.at[:, lanes], values_ref.at[:, lanes], value_sems.at[q])
 
     late = [
@@ -195,7 +202,7 @@
             weight_hbm.at[:, pl.ds(d * cols, cols)], tiles_ref.at[d], tile_sems.at[d]
         )
 
-    for q in range(chunks // 2):
+    for q in range(groups):
         value_copy(q).start()
     for copy in late_copies:
         copy.start()
@@ -272,13 +279,11 @@
     before_logs[...] = jnp.zeros_like(before_logs)
 
     def state_of(q):
-        lanes = slice(2 * q * CHUNK, 2 * (q + 1) * CHUNK)
+        lanes = group_lanes(q)
         value_copy(q).wait()
         wide = dot(wide_ref[...], expander_ref[:, lanes])
         scaled = (wide * values_ref[:, lanes].astype(F32)).astype(BF16)
-        state = dot(turned_ref[...], scaled).astype(BF16)
-        mine_state[2 * q] = state[:, :CHUNK]
-        mine_state[2 * q + 1] = state[:, CHUNK:]
+        mine_state[:, lanes] = dot(turned_ref[...], scaled).astype(BF16)
 
     state_of(0)
 
@@ -306,7 +311,7 @@
 
     def pair_copy(c):
         return remote(
-            mine_state.at[c, other_rows],
+            mine_state.at[other_rows, some_lanes(c)],
             pair_state.at[c],
             pair_ssems.at[c],
             pair_rsems.at[c],
@@ -325,7 +330,7 @@
     def swap_copy(c, where):
         return remote(
             swap_ref.at[c],
-            enter_ref.at[c, where],
+            enter_ref.at[where, some_lanes(c)],
             swap_ssems.at[c],
             swap_rsems.at[c],
             {"ctx": mate(0)},
@@ -368,7 +373,7 @@
 
     def pair_up(c):
         pair_copy(c).wait_recv()
-        mine = mine_state[c, own_rows].astype(F32)
+        mine = mine_state[own_rows, lanes_of(c)].astype(F32)
         theirs = pair_state[c].astype(F32)
         first, second = jnp.where(odd, theirs, mine), jnp.where(odd, mine, theirs)
         totals[0, c] = (first * pair_scale[0:1, lanes_of(c)] + second).astype(BF16)
@@ -378,19 +383,23 @@
             scan_copy(1, c).start()
 
     pairs = chunks // 2
-    for q in range(pairs):
+
+    def group_order(q):
+        return sorted(range(q * GROUP, (q + 1) * GROUP), key=lambda c: 1 - c % 2)
+
+    for q in range(groups):
         if q:
             state_of(q)
-        pair_copy(2 * q + 1).start()
-        pair_copy(2 * q).start()
+        for c in group_order(q):
+            pair_copy(c).start()
         if q == 1:
             exchange_logs(0)
         if q > 1:
-            pair_up(2 * q - 3)
-            pair_up(2 * q - 4)
-    for q in range(pairs - 2, pairs):
-        pair_up(2 * q + 1)
-        pair_up(2 * q)
+            for c in group_order(q - 2):
+                pair_up(c)
+    for q in range(groups - 2, groups):
+        for c in group_order(q):
+            pair_up(c)
     if squared:
         for c in range(0, chunks, 2):
 
@@ -399,9 +408,9 @@
                 scan_copy(1, c).start()
 
     def enter(c, before):
-        even_state = jnp.where(odd, pair_state[c].astype(F32), mine_state[c, own_rows].astype(F32))
+        even_state = jnp.where(odd, pair_state[c].astype(F32), mine_state[own_rows, some_lanes(c)].astype(F32))
         moved = before * pair_scale[1:2, some_lanes(c)] + even_state
-        enter_ref[c, own_rows] = jnp.where(odd, moved, before).astype(BF16)
+        enter_ref[own_rows, some_lanes(c)] = jnp.where(odd, moved, before).astype(BF16)
         swap_ref[c] = jnp.where(odd, before, moved).astype(BF16)
         swap_copy(c, own_rows).start()
 
@@ -450,7 +459,7 @@
         first = [(q, cross_row, q) for q in range(pairs)]
         first += [(q + pairs, end_row, q) for q in range(pairs)]
         second = [(q, next_row, q) for q in range(pairs)]
-        second += [(q + 2.5, last_column, q) for q in range(pairs)]
+        second += [(q + 4.5, last_column, q) for q in range(pairs)]
         return [sorted(events, key=lambda event: event[0]) for events in (first, second)]
 
     def run_events(here, events):
@@ -561,7 +570,7 @@
         if hook is not None:
             hook(HOOKS * b + 2)
         offset = offset_ref[0:1, :]
-        gain_ref[span, :] = (opened * spread(jnp.exp(running_t + offset), expander)).astype(BF16)
+        gate_ref[span, :] = (opened * spread(jnp.exp(running_t + offset), expander)).astype(BF16)
         offset_ref[0:1, :] = offset + running_t[BLOCK - 1 : BLOCK, :]
         scaled = (spread(jnp.exp(after) * turned, expander) * values).astype(BF16)
         state_ref[...] = state_ref[...] * decay[BLOCK - 1 : BLOCK, :] + dot(
@@ -572,8 +581,7 @@
 
     def hook(g):
         if squared:
-            if g in (0, 1, 3):
-                run_events(row == 0, square_events()[0][g - g // 3 : g - g // 3 + 1])
+            run_events(row == 0, square_events()[0][g : g + 1])
             return
 
         for s in range(2, levels + 1):
@@ -606,7 +614,7 @@
     block_local(0, hook)
     if squared:
         first, second = square_events()
-        run_events(row == 0, first[HOOKS - 1 :])
+        run_events(row == 0, first[HOOKS:])
         run_events(row == 1, second)
     else:
         lax.fori_loop(HOOKS, max(chunks + LAG * (levels - 1), HOOKS), late_round, 0)
@@ -615,8 +623,9 @@
     for d in range(n):
         tile_copy(d).wait()
 
-    def share(rows, d):
-        return dot(normed_ref[rows, :], tiles_ref[d])
+    def share(d, q):
+        rows = rows_of(q // PARTS)
+        return dot(normed_ref[rows, :], tiles_ref[d, :, pl.ds(pl.multiple_of(q % PARTS * part, part), part)])
 
     def hop_up(d, b):
         return remote(
@@ -654,7 +663,7 @@
         return pl.ds(pl.multiple_of(b * BLOCK, BLOCK), BLOCK)
 
     def pass_on(d, b, slot, move, fed):
-        acc_ref[...] = share(rows_of(b), d)
+        acc_ref[...] = share(d, b)
 
         @pl.when(fed)
         def _():
@@ -668,10 +677,11 @@
         span = rows_of(b)
         readout = read_ref[span, :]
         pieces = []
-        for c in range(chunks):
-            arrival = dot(readout, enter_ref[c])
-            piece = normed_ref[span, lanes_of(c)].astype(F32)
-            pieces.append(piece + arrival * gain_ref[span, lanes_of(c)].astype(F32))
+        for q in range(groups):
+            lanes = group_lanes(q)
+            arrival = dot(readout, enter_ref[:, lanes])
+            piece = normed_ref[span, lanes].astype(F32)
+            pieces.append(piece + arrival * gate_ref[span, lanes].astype(F32))
         normed_ref[span, :] = finish_rows(jnp.concatenate(pieces, axis=1), norm_ref[...])
 
     padded = slocal_ref.shape[0]
@@ -683,13 +693,14 @@
         for p in range(peers - 1):
             picked_copy(p).wait_recv()
         asked = picked_all[...].reshape(peers * padded, entries)
-        for c in range(chunks):
-            final = enter_ref[c].astype(F32) * pair_scale[0:1, lanes_of(c)] + mine_state[c].astype(F32)
+        for q in range(groups):
+            lanes = group_lanes(q)
+            entered = enter_ref[:, lanes].astype(F32) * pair_scale[0:1, lanes]
+            final = entered + mine_state[:, lanes].astype(F32)
             told = dot(asked, final.astype(BF16))
             for p in range(peers - 1):
-                reply_ref[p, :, lanes_of(c)] = told[p * padded : p * padded + few_rows]
-            own = told[last_seat * padded : last_seat * padded + few_rows]
-            reply_got[:, lanes_of(c)] = own
+                reply_ref[p, :, lanes] = told[p * padded : p * padded + few_rows]
+            reply_got[:, lanes] = told[last_seat * padded : last_seat * padded + few_rows]
         for p in range(peers - 1):
             reply_copy(p).start()
 
@@ -707,7 +718,7 @@
     few = sresult_ref.shape[0]
 
     def sshare(d):
-        wide = share(srows, d)
+        wide = dot(normed_ref[srows, :], tiles_ref[d])
         return jnp.concatenate([wide[:few, q * LANES : (q + 1) * LANES] for q in range(cols // LANES)], axis=0)
 
     def spass_on(d, slot, move, fed):
@@ -721,27 +732,31 @@
         ssent[d] = sown_ref[...].astype(BF16)
         move(d).start()
 
+    sample_start = PARTS * (blocks + 1)
+
     def step(t, carry):
-        @pl.when(t < blocks)
-        def _():
-            finish_block(t)
-
-        @pl.when(t == blocks + 1)
+        block, first_part, last_part = t // PARTS, t % PARTS == 0, t % PARTS == PARTS - 1
+
+        @pl.when((block < blocks) & first_part)
+        def _():
+            finish_block(block)
+
+        @pl.when(t == sample_start)
         def _():
             finish_samples()
 
         rising, falling = t - place, t - (n - 1 - place)
-        up, down = n - 1 - rising // blocks, falling // blocks
+        up, down = n - 1 - rising // per, falling // per
 
         @pl.when((rising >= 0) & (up > place))
         def _():
-            pass_on(up, rising % blocks, up + 1, hop_up, place > 0)
+            pass_on(up, rising % per, up + 1, hop_up, place > 0)
 
         @pl.when((falling >= 0) & (down < place))
         def _():
-            pass_on(down, falling % blocks, down, hop_down, place < n - 1)
-
-        srising, sfalling = rising - (blocks + 1), falling - (blocks + 1)
+            pass_on(down, falling % per, down, hop_down, place < n - 1)
+
+        srising, sfalling = rising - sample_start, falling - sample_start
         sup, sdown = n - 1 - srising, sfalling
 
         @pl.when((srising >= 0) & (sup > place))
@@ -752,11 +767,11 @@
         def _():
             spass_on(sdown, sdown, shop_down, place < n - 1)
 
-        @pl.when(t + 1 < blocks)
-        def _():
-            block_local(t + 1, None)
-
-        @pl.when(t == blocks - 2)
+        @pl.when((block + 1 < blocks) & last_part)
+        def _():
+            block_local(block + 1, None)
+
+        @pl.when((block == blocks - 2) & last_part)
         def _():
             sample_local()
 
@@ -764,20 +779,14 @@
             def _():
                 picked_copy(seat).start()
 
-        @pl.when((t == blocks - 1) & holds_final)
+        @pl.when((block == blocks - 1) & last_part & holds_final)
         def _():
             answer()
 
         return carry
 
-    lax.fori_loop(0, (n - 1) * blocks, step, 0)
+    lax.fori_loop(0, (n - 1) * per, step, 0)
     sown_ref[...] = sshare(place)
-
-    def own(b, carry):
-        own_ref[b] = share(rows_of(b), place)
-        return carry
-
-    lax.fori_loop(0, blocks, own, 0)
 
     @pl.when(place < n - 1)
     def _():
@@ -794,33 +803,6 @@
     sout_copy = pltpu.make_async_copy(sresult_ref, sout_hbm, late_sems.at[len(late)])
     sout_copy.start()
 
-    def drain(t, carry):
-        d, b = t // blocks, t % blocks
-
-        @pl.when(d > place)
-        def _():
-            hop_up(d, b).wait_send()
-
-        @pl.when(d < place)
-        def _():
-            hop_down(d, b).wait_send()
-
-        return carry
-
-    lax.fori_loop(0, n * blocks, drain, 0)
-
-    def sdrain(d, carry):
-        @pl.when(d > place)
-        def _():
-            shop_up(d).wait_send()
-
-        @pl.when(d < place)
-        def _():
-            shop_down(d).wait_send()
-
-        return carry
-
-    lax.fori_loop(0, n, sdrain, 0)
     for c in range(chunks):
         pair_copy(c).wait_send()
         swap_copy(c, own_rows).wait_send()
@@ -840,33 +822,72 @@
     @pl.when(jnp.logical_not(holds_final))
     def _():
         picked_copy(seat).wait_send()
+
     def out_copy(b):
         return pltpu.make_async_copy(
             result_ref.at[b],
-            out_hbm.at[:, pl.ds(pl.multiple_of(b * BLOCK, BLOCK), BLOCK)],
+            out_hbm.at[pl.ds(pl.multiple_of(b % PARTS * part, part), part), rows_of(b // PARTS)],
             out_sems.at[b],
         )
 
     def gather(b, carry):
+        acc_ref[...] = share(place, b)
+
         @pl.when(place < n - 1)
         def _():
             hop_down(place, b).wait_recv()
-            own_ref[b] = own_ref[b] + landing[place, b].astype(F32)
+            acc_ref[...] = acc_ref[...] + landing[place, b].astype(F32)
 
         @pl.when(place > 0)
         def _():
             hop_up(place, b).wait_recv()
-            own_ref[b] = own_ref[b] + landing[place + 1, b].astype(F32)
-
-        result_ref[b] = turn_over(own_ref[b]).astype(BF16)
+            acc_ref[...] = acc_ref[...] + landing[place + 1, b].astype(F32)
+
+        result_ref[b] = turn_over(acc_ref[...]).astype(BF16)
         out_copy(b).start()
+        for d in range(n):
+
+            @pl.when(d > place)
+            def _():
+                hop_up(d, b).wait_send()
+
+            @pl.when(d < place)
+            def _():
+                hop_down(d, b).wait_send()
+
         return carry
 
-    lax.fori_loop(0, blocks, gather, 0)
+    lax.fori_loop(0, per, gather, 0)
+    for d in range(n):
+
+        @pl.when(d > place)
+        def _():
+            shop_up(d).wait_send()
+
+        @pl.when(d < place)
+        def _():
+            shop_down(d).wait_send()
 
     sout_copy.wait()
-    for b in range(blocks):
+    for b in range(per):
         out_copy(b).wait()
+
+
+def hand_over_kernel(bands, mixed_hbm, smixed_hbm, out_hbm, sout_hbm, bands_ref, few_ref, sems):
+    rows = mixed_hbm.shape[0] // bands
+    moves = [(smixed_hbm, few_ref, sout_hbm)]
+    for q in range(bands):
+        part = pl.ds(q * rows, rows)
+        moves.append((mixed_hbm.at[part], bands_ref.at[q], out_hbm.at[part]))
+    ins = [pltpu.make_async_copy(a, b, sems.at[0, q]) for q, (a, b, _) in enumerate(moves)]
+    outs = [pltpu.make_async_copy(b, c, sems.at[1, q]) for q, (_, b, c) in enumerate(moves)]
+    for copy in ins:
+        copy.start()
+    for into, out in zip(ins, outs):
+        into.wait()
+        out.start()
+    for copy in outs:
+        copy.wait()
 
 
 def per_device(
@@ -898,6 +919,7 @@
     padded = -(-samples // (2 * PAD)) * 2 * PAD
     cols = out_weight.shape[1] // n
     blocks, chunks = tokens // BLOCK, channels // CHUNK
+    part, per = cols // PARTS, blocks * PARTS
     vmem = pl.BlockSpec(memory_space=pltpu.VMEM)
     hbm = pl.BlockSpec(memory_space=pl.ANY)
     dma = pltpu.SemaphoreType.DMA
@@ -940,13 +962,13 @@
             V((2 * heads, channels), BF16),
             V((entries, tokens), BF16),
             V((PAD, channels), F32),
-            V((chunks, entries, CHUNK), BF16),
+            V((entries, channels), BF16),
             V((chunks, half, CHUNK), BF16),
             V((levels + 1, chunks, half, CHUNK), BF16),
             V((scan_steps, chunks, half, CHUNK), BF16),
             V((chunks, half, CHUNK), F32),
             V((chunks, half, CHUNK), BF16),
-            V((chunks, entries, CHUNK), BF16),
+            V((entries, channels), BF16),
             V((levels + 1, PAD, heads), F32),
             V((levels + 1, PAD, heads), F32),
             V((PAD, heads), F32),
@@ -955,7 +977,6 @@
             V((entries, channels), F32),
             V((PAD, heads), F32),
             V((BLOCK, channels), F32),
-            V((tokens, channels), BF16),
             V((tokens + padded, channels), BF16),
             V((padded, channels), F32),
             V((padded, channels), F32),
@@ -963,19 +984,18 @@
             V((peers, padded, entries), BF16),
             V((peers - 1, -(-samples // PAD) * PAD, channels), F32),
             V((-(-samples // PAD) * PAD, channels), F32),
-            V((BLOCK, cols), F32),
-            V((blocks, BLOCK, cols), F32),
-            V((n, blocks, BLOCK, cols), BF16),
-            V((n + 1, blocks, BLOCK, cols), BF16),
+            V((BLOCK, part), F32),
+            V((n, per, BLOCK, part), BF16),
+            V((n + 1, per, BLOCK, part), BF16),
             V((n, samples * cols // LANES, LANES), BF16),
             V((n + 1, samples * cols // LANES, LANES), BF16),
             V((samples * cols // LANES, LANES), F32),
-            V((blocks, cols, BLOCK), BF16),
+            V((per, part, BLOCK), BF16),
             V((samples, cols), BF16),
             dma((chunks,)),
             dma((8,)),
             dma((n,)),
-            dma((blocks,)),
+            dma((per,)),
             dma((levels + 1,)),
             dma((levels + 1,)),
             dma((chunks,)),
@@ -988,8 +1008,8 @@
             dma((1,)),
             dma((peers,)),
             dma((peers,)),
-            dma((n, blocks)),
-            dma((n + 1, blocks)),
+            dma((n, per)),
+            dma((n + 1, per)),
             dma((n,)),
             dma((n + 1,)),
         ],
@@ -1013,6 +1033,19 @@
         sample_read.reshape(samples, length, entries),
         sample_step.transpose(1, 2, 0),
     )
+    bands = 4
+    band = (cols // bands, tokens)
+    mixed, smixed = pl.pallas_call(
+        functools.partial(hand_over_kernel, bands),
+        out_shape=(shape((cols, tokens), BF16), shape((samples, cols), BF16)),
+        in_specs=[hbm, hbm],
+        out_specs=(hbm, hbm),
+        scratch_shapes=[
+            V((bands, *band), BF16),
+            V((samples, cols), BF16),
+            dma((2, bands + 1)),
+        ],
+    )(mixed, smixed)
     return mixed, smixed.T
 
 

time: 97.8 us -> 97.4 us (level)
  local copies, waits for them, and re-layouts: 2.86 us -> 0 us
  Pallas kernels: 93.9 us -> 96.4 us
    unnamed x4 -> x0, local copies, waits for them, and re-layouts: 2.86 us -> none
    pallas_call x0 -> x1, Pallas kernels: none -> 2 us  [per_device(): pl.pallas_call(functools.partial(hand_over_kernel, bands), out_shape=(sha...]
where the time goes in v5:
time: 97.4 us; the launch traced here: 97.2 us
  Pallas kernels  96.4 us (99%)
    pallas_call x1, Pallas kernels, per_device(): pl.pallas_call(functools.partial(layer_kernel, dim, n, peers), out_shape=...  94.4 us
    pallas_call x1, Pallas kernels, per_device(): pl.pallas_call(functools.partial(hand_over_kernel, bands), out_shape=(sha...  2 us

profile of v5, /device:TPU:21, one launch (start us, length us, event | category | flops | bytes accessed | tf_op | source)
XLA Modules:
  0.0 97.2 jit_solution(6058919968673907411)
XLA Ops:
  0.6 94.4 %shard_map.158 = (bf16[1024,512]{1,0:T(8,128)(2,1)}, bf16[2,1024]{1,0:T(2,128)(2,1)}) custom-call(s32[2]{0:T(128)} %length_ref.1, bf16[512,2048]{1,0:T(8,128)(2,1)} %values_hbm.1, bf16[512,2048]{1,0:T(8,128)(2,1)} %gate_hbm.1, bf16[512,256]{1,0:T(8,128)(2,1)} %bitcast.9, bf16[512,256]{1,0:T(8,128)(2,1)} %bitcast.10, f32[32,512]{1,0:T(8,128)} %step_ref.1, ...), custom_call_target="tpu_custom_call" | custom-call | tf_op jit(solution)/shard_map/pallas_call | solution.py:928
  95.0 2.0 %shard_map.159 = (bf16[1024,512]{1,0:T(8,128)(2,1)}, bf16[2,1024]{1,0:T(2,128)(2,1)}) custom-call(bf16[1024,512]{1,0:T(8,128)(2,1)} %get-tuple-element.6.mixed_hbm, bf16[2,1024]{1,0:T(2,128)(2,1)} %get-tuple-element.7.smixed_hbm), custom_call_target="tpu_custom_call" | custom-call | tf_op jit(solution)/shard_map/pallas_call | solution.py:1038

commit v6 on v5

--- a/solution.py
+++ b/solution.py
@@ -197,10 +197,7 @@
     ]
     late_copies = [pltpu.make_async_copy(*refs, late_sems.at[q]) for q, refs in enumerate(late)]
 
-    def tile_copy(d):
-        return pltpu.make_async_copy(
-            weight_hbm.at[:, pl.ds(d * cols, cols)], tiles_ref.at[d], tile_sems.at[d]
-        )
+    tile_copy = pltpu.make_async_copy(weight_hbm, tiles_ref, tile_sems.at[0])
 
     for q in range(groups):
         value_copy(q).start()
@@ -309,12 +306,12 @@
             log_sent.at[s], log_got.at[s], log_ssems.at[s], log_rsems.at[s], {"ctx": mate(s)}
         )
 
-    def pair_copy(c):
-        return remote(
-            mine_state.at[other_rows, some_lanes(c)],
-            pair_state.at[c],
-            pair_ssems.at[c],
-            pair_rsems.at[c],
+    def pair_copy(q):
+        return remote(
+            mine_state.at[other_rows, group_lanes(q)],
+            pair_state.at[:, group_lanes(q)],
+            pair_ssems.at[0],
+            pair_rsems.at[q],
             {"ctx": mate(0)},
         )
 
@@ -322,17 +319,17 @@
         return remote(
             totals.at[s - 1, c],
             arrived.at[s - 1, c],
-            scan_ssems.at[s - 1, c],
+            scan_ssems.at[s - 1],
             scan_rsems.at[s - 1, c],
             {"ctx": mate(1 if squared and s == 3 else s)},
         )
 
-    def swap_copy(c, where):
-        return remote(
-            swap_ref.at[c],
-            enter_ref.at[where, some_lanes(c)],
-            swap_ssems.at[c],
-            swap_rsems.at[c],
+    def swap_copy(lanes, where):
+        return remote(
+            swap_ref.at[:, lanes],
+            enter_ref.at[where, lanes],
+            swap_ssems.at[0],
+            swap_rsems.at[0],
             {"ctx": mate(0)},
         )
 
@@ -364,17 +361,9 @@
             return column == 0
         return (column == 1) & (row == 0)
 
-    def sends(s, c):
-        if not squared:
-            return seat >= 0
-        if s == 1:
-            return column == 0 if c % 2 else row == 0
-        return (column == c % 2) & (row == s - 2)
-
     def pair_up(c):
-        pair_copy(c).wait_recv()
         mine = mine_state[own_rows, lanes_of(c)].astype(F32)
-        theirs = pair_state[c].astype(F32)
+        theirs = pair_state[:, lanes_of(c)].astype(F32)
         first, second = jnp.where(odd, theirs, mine), jnp.where(odd, mine, theirs)
         totals[0, c] = (first * pair_scale[0:1, lanes_of(c)] + second).astype(BF16)
 
@@ -384,22 +373,21 @@
 
     pairs = chunks // 2
 
-    def group_order(q):
-        return sorted(range(q * GROUP, (q + 1) * GROUP), key=lambda c: 1 - c % 2)
+    def pair_group(q):
+        pair_copy(q).wait_recv()
+        for c in sorted(range(q * GROUP, (q + 1) * GROUP), key=lambda c: 1 - c % 2):
+            pair_up(c)
 
     for q in range(groups):
         if q:
             state_of(q)
-        for c in group_order(q):
-            pair_copy(c).start()
+        pair_copy(q).start()
         if q == 1:
             exchange_logs(0)
         if q > 1:
-            for c in group_order(q - 2):
-                pair_up(c)
+            pair_group(q - 2)
     for q in range(groups - 2, groups):
-        for c in group_order(q):
-            pair_up(c)
+        pair_group(q)
     if squared:
         for c in range(0, chunks, 2):
 
@@ -408,11 +396,11 @@
                 scan_copy(1, c).start()
 
     def enter(c, before):
-        even_state = jnp.where(odd, pair_state[c].astype(F32), mine_state[own_rows, some_lanes(c)].astype(F32))
+        even_state = jnp.where(odd, pair_state[:, some_lanes(c)].astype(F32), mine_state[own_rows, some_lanes(c)].astype(F32))
         moved = before * pair_scale[1:2, some_lanes(c)] + even_state
         enter_ref[own_rows, some_lanes(c)] = jnp.where(odd, moved, before).astype(BF16)
-        swap_ref[c] = jnp.where(odd, before, moved).astype(BF16)
-        swap_copy(c, own_rows).start()
+        swap_ref[:, some_lanes(c)] = jnp.where(odd, before, moved).astype(BF16)
+        swap_copy(some_lanes(c), own_rows).start()
 
     def cross_row(q):
         c = 2 * q + column
@@ -528,9 +516,7 @@
     offset_ref[...] = jnp.zeros_like(offset_ref)
     for copy in late_copies:
         copy.wait()
-    for k in range((n + 1) // 2):
-        for d in sorted({n - 1 - k, k}, reverse=True):
-            tile_copy(d).start()
+    tile_copy.start()
 
     def block_local(b, hook):
         span = pl.ds(pl.multiple_of(b * BLOCK, BLOCK), BLOCK)
@@ -599,12 +585,12 @@
 
     def picked_copy(p):
         return remote(
-            picked_ref, picked_all.at[p], small_ssems.at[0], picked_sems.at[p], {"ctx": last_seat}
+            picked_ref, picked_all.at[p], small_ssems.at[0], picked_sems.at[0], {"ctx": last_seat}
         )
 
     def reply_copy(p):
         return remote(
-            reply_ref.at[p], reply_got, reply_sems.at[p], small_rsems.at[0], {"ctx": p}
+            reply_ref.at[p], reply_got, reply_sems.at[0], small_rsems.at[0], {"ctx": p}
         )
 
     def late_round(g, carry):
@@ -618,20 +604,19 @@
         run_events(row == 1, second)
     else:
         lax.fori_loop(HOOKS, max(chunks + LAG * (levels - 1), HOOKS), late_round, 0)
-    for c in range(chunks):
-        swap_copy(c, other_rows).wait_recv()
-    for d in range(n):
-        tile_copy(d).wait()
+    swap_copy(slice(0, channels), other_rows).wait_recv()
+    tile_copy.wait()
 
     def share(d, q):
         rows = rows_of(q // PARTS)
-        return dot(normed_ref[rows, :], tiles_ref[d, :, pl.ds(pl.multiple_of(q % PARTS * part, part), part)])
+        start = pl.multiple_of(d * cols + q % PARTS * part, part)
+        return dot(normed_ref[rows, :], tiles_ref[:, pl.ds(start, part)])
 
     def hop_up(d, b):
         return remote(
             sent.at[d, b],
             landing.at[d + 1, b],
-            sent_sems.at[d, b],
+            sent_sems.at[d],
             land_sems.at[d + 1, b],
             {"head": place + 1},
         )
@@ -640,9 +625,19 @@
         return remote(
             sent.at[d, b],
             landing.at[d, b],
-            sent_sems.at[d, b],
+            sent_sems.at[d],
             land_sems.at[d, b],
             {"head": place - 1},
+        )
+
+    def all_up(d):
+        return remote(
+            sent.at[d], landing.at[d + 1], sent_sems.at[d], land_sems.at[0, 0], {"head": place + 1}
+        )
+
+    def all_down(d):
+        return remote(
+            sent.at[d], landing.at[d], sent_sems.at[d], land_sems.at[0, 0], {"head": place - 1}
         )
 
     def shop_up(d):
@@ -690,8 +685,8 @@
 
     def answer():
         picked_all[last_seat] = picked_ref[...]
-        for p in range(peers - 1):
-            picked_copy(p).wait_recv()
+        others = picked_all.at[pl.ds(0, peers - 1)]
+        remote(others, others, small_ssems.at[0], picked_sems.at[0], {"ctx": 0}).wait_recv()
         asked = picked_all[...].reshape(peers * padded, entries)
         for q in range(groups):
             lanes = group_lanes(q)
@@ -718,7 +713,7 @@
     few = sresult_ref.shape[0]
 
     def sshare(d):
-        wide = dot(normed_ref[srows, :], tiles_ref[d])
+        wide = dot(normed_ref[srows, :], tiles_ref[:, pl.ds(pl.multiple_of(d * cols, cols), cols)])
         return jnp.concatenate([wide[:few, q * LANES : (q + 1) * LANES] for q in range(cols // LANES)], axis=0)
 
     def spass_on(d, slot, move, fed):
@@ -803,32 +798,53 @@
     sout_copy = pltpu.make_async_copy(sresult_ref, sout_hbm, late_sems.at[len(late)])
     sout_copy.start()
 
-    for c in range(chunks):
-        pair_copy(c).wait_send()
-        swap_copy(c, own_rows).wait_send()
-        for s in range(1, scan_steps + 1):
-
-            @pl.when(sends(s, c))
+    remote(
+        mine_state.at[other_rows], pair_state, pair_ssems.at[0], pair_rsems.at[0], {"ctx": mate(0)}
+    ).wait_send()
+    swap_copy(slice(0, channels), own_rows).wait_send()
+
+    def scan_sent(s, count):
+        span = pl.ds(0, count)
+        remote(
+            totals.at[s - 1, span],
+            arrived.at[s - 1, span],
+            scan_ssems.at[s - 1],
+            scan_rsems.at[s - 1, 0],
+            {"ctx": mate(1)},
+        ).wait_send()
+
+    for s in range(1, scan_steps + 1):
+        if not squared:
+            scan_sent(s, chunks)
+        elif s == 1:
+
+            @pl.when((column == 0) & (row == 0))
             def _():
-                scan_copy(s, c).wait_send()
+                scan_sent(1, chunks)
+
+            @pl.when(column + row == 1)
+            def _():
+                scan_sent(1, pairs)
+
+        else:
+
+            @pl.when(row == s - 2)
+            def _():
+                scan_sent(s, pairs)
+
     for s in range(log_steps):
         log_copy(s).wait_send()
 
     @pl.when(holds_final)
     def _():
-        for p in range(peers - 1):
-            reply_copy(p).wait_send()
+        remote(reply_ref, reply_ref, reply_sems.at[0], small_rsems.at[0], {"ctx": 0}).wait_send()
 
     @pl.when(jnp.logical_not(holds_final))
     def _():
         picked_copy(seat).wait_send()
 
-    def out_copy(b):
-        return pltpu.make_async_copy(
-            result_ref.at[b],
-            out_hbm.at[pl.ds(pl.multiple_of(b % PARTS * part, part), part), rows_of(b // PARTS)],
-            out_sems.at[b],
-        )
+    def out_place(b):
+        return pl.ds(pl.multiple_of(b % PARTS * part, part), part), rows_of(b // PARTS)
 
     def gather(b, carry):
         acc_ref[...] = share(place, b)
@@ -843,18 +859,9 @@
             hop_up(place, b).wait_recv()
             acc_ref[...] = acc_ref[...] + landing[place + 1, b].astype(F32)
 
-        result_ref[b] = turn_over(acc_ref[...]).astype(BF16)
-        out_copy(b).start()
-        for d in range(n):
-
-            @pl.when(d > place)
-            def _():
-                hop_up(d, b).wait_send()
-
-            @pl.when(d < place)
-            def _():
-                hop_down(d, b).wait_send()
-
+        where = out_place(b)
+        result_ref[where] = turn_over(acc_ref[...]).astype(BF16)
+        pltpu.make_async_copy(result_ref.at[where], out_hbm.at[where], out_sems.at[0]).start()
         return carry
 
     lax.fori_loop(0, per, gather, 0)
@@ -862,15 +869,16 @@
 
         @pl.when(d > place)
         def _():
+            all_up(d).wait_send()
             shop_up(d).wait_send()
 
         @pl.when(d < place)
         def _():
+            all_down(d).wait_send()
             shop_down(d).wait_send()
 
     sout_copy.wait()
-    for b in range(per):
-        out_copy(b).wait()
+    pltpu.make_async_copy(result_ref, out_hbm, out_sems.at[0]).wait()
 
 
 def hand_over_kernel(bands, mixed_hbm, smixed_hbm, out_hbm, sout_hbm, bands_ref, few_ref, sems):
@@ -910,6 +918,7 @@
     n, peers = lax.axis_size("head"), lax.axis_size("ctx")
     levels = peers.bit_length() - 2
     scan_steps = 3 if levels == 2 else levels
+    log_steps = 2 if levels == 2 else levels + 1
     tokens, channels = prompt_values.shape
     heads = prompt_step.shape[0]
     dim = channels // heads
@@ -955,7 +964,7 @@
             V((samples, length, entries), BF16),
             V((samples, length, entries), BF16),
             V((samples, length, heads), F32),
-            V((n, channels, cols), BF16),
+            V(out_weight.shape, BF16),
             V((blocks, heads, BLOCK), F32),
             V((blocks, heads, BLOCK), F32),
             V((tokens, 2 * heads), BF16),
@@ -963,14 +972,14 @@
             V((entries, tokens), BF16),
             V((PAD, channels), F32),
             V((entries, channels), BF16),
-            V((chunks, half, CHUNK), BF16),
+            V((half, channels), BF16),
             V((levels + 1, chunks, half, CHUNK), BF16),
             V((scan_steps, chunks, half, CHUNK), BF16),
             V((chunks, half, CHUNK), F32),
-            V((chunks, half, CHUNK), BF16),
+            V((half, channels), BF16),
             V((entries, channels), BF16),
-            V((levels + 1, PAD, heads), F32),
-            V((levels + 1, PAD, heads), F32),
+            V((log_steps, PAD, heads), F32),
+            V((log_steps, PAD, heads), F32),
             V((PAD, heads), F32),
             V((PAD, channels), F32),
             V((levels, PAD, channels), F32),
@@ -990,25 +999,25 @@
             V((n, samples * cols // LANES, LANES), BF16),
             V((n + 1, samples * cols // LANES, LANES), BF16),
             V((samples * cols // LANES, LANES), F32),
-            V((per, part, BLOCK), BF16),
+            V((cols, tokens), BF16),
             V((samples, cols), BF16),
-            dma((chunks,)),
+            dma((chunks // GROUP,)),
             dma((8,)),
-            dma((n,)),
-            dma((per,)),
-            dma((levels + 1,)),
-            dma((levels + 1,)),
-            dma((chunks,)),
-            dma((chunks,)),
-            dma((scan_steps, chunks)),
-            dma((scan_steps, chunks)),
-            dma((chunks,)),
-            dma((chunks,)),
             dma((1,)),
             dma((1,)),
-            dma((peers,)),
-            dma((peers,)),
-            dma((n, per)),
+            dma((log_steps,)),
+            dma((log_steps,)),
+            dma((1,)),
+            dma((chunks // GROUP,)),
+            dma((scan_steps,)),
+            dma((scan_steps, chunks)),
+            dma((1,)),
+            dma((1,)),
+            dma((1,)),
+            dma((1,)),
+            dma((1,)),
+            dma((1,)),
+            dma((n,)),
             dma((n + 1, per)),
             dma((n,)),
             dma((n + 1,)),

time: 97.4 us -> 95.9 us (0.985)
  Pallas kernels: 96.4 us -> 94.9 us
    pallas_call x1, Pallas kernels: 94.4 us -> 92.9 us  [per_device(): pl.pallas_call(functools.partial(layer_kernel, dim, n, peers), out_shape=...]
where the time goes in v6:
time: 95.9 us; the launch traced here: 95.7 us
  Pallas kernels  94.9 us (99%)
    pallas_call x1, Pallas kernels, per_device(): pl.pallas_call(functools.partial(layer_kernel, dim, n, peers), out_shape=...  92.9 us
    pallas_call x1, Pallas kernels, per_device(): pl.pallas_call(functools.partial(hand_over_kernel, bands), out_shape=(sha...  2 us

profile of v6, /device:TPU:21, one launch (start us, length us, event | category | flops | bytes accessed | tf_op | source)
XLA Modules:
  0.0 95.7 jit_solution(780051405866801382)
XLA Ops:
  0.6 92.9 %shard_map.158 = (bf16[1024,512]{1,0:T(8,128)(2,1)}, bf16[2,1024]{1,0:T(2,128)(2,1)}) custom-call(s32[2]{0:T(128)} %length_ref.1, bf16[512,2048]{1,0:T(8,128)(2,1)} %values_hbm.1, bf16[512,2048]{1,0:T(8,128)(2,1)} %gate_hbm.1, bf16[512,256]{1,0:T(8,128)(2,1)} %bitcast.9, bf16[512,256]{1,0:T(8,128)(2,1)} %bitcast.10, f32[32,512]{1,0:T(8,128)} %step_ref.1, ...), custom_call_target="tpu_custom_call" | custom-call | tf_op jit(solution)/shard_map/pallas_call | solution.py:937
  93.5 2.0 %shard_map.159 = (bf16[1024,512]{1,0:T(8,128)(2,1)}, bf16[2,1024]{1,0:T(2,128)(2,1)}) custom-call(bf16[1024,512]{1,0:T(8,128)(2,1)} %get-tuple-element.6.mixed_hbm, bf16[2,1024]{1,0:T(2,128)(2,1)} %get-tuple-element.7.smixed_hbm), custom_call_target="tpu_custom_call" | custom-call | tf_op jit(solution)/shard_map/pallas_call | solution.py:1047

commit v7 on v6

--- a/solution.py
+++ b/solution.py
@@ -201,8 +201,6 @@
 
     for q in range(groups):
         value_copy(q).start()
-    for copy in late_copies:
-        copy.start()
 
     def digit(s):
         return (seat // (1 << s)) % 2
@@ -251,17 +249,24 @@
         expander_ref[...] = expander_of(heads, dim)
 
     fill_expander()
-    later = jnp.zeros((heads, 1), F32)
+    def stack(ref, wide):
+        for b in range(blocks):
+            ref[b] = wide[:, b * BLOCK : (b + 1) * BLOCK]
+        return ref[...].reshape(blocks * heads, BLOCK)
+
+    tall_steps, tall_logs = stack(steps_ref, steps), stack(logs_ref, logs)
+    after = dot(tall_logs, jnp.where(i > j, 1.0, 0.0), precision=EXACT)
+    sums = jnp.sum(tall_logs, axis=1, keepdims=True)
+    later, offsets = jnp.zeros((heads, 1), F32), []
     for b in reversed(range(blocks)):
-        span = slice(b * BLOCK, (b + 1) * BLOCK)
-        steps_ref[b] = steps[:, span]
-        logs_ref[b] = logs[:, span]
-        after = dot(logs[:, span], jnp.where(i > j, 1.0, 0.0), precision=EXACT) + later
-        later = later + jnp.sum(logs[:, span], axis=1, keepdims=True)
-        w = turn_over(jnp.exp(after) * steps[:, span])
-        high = w.astype(BF16)
-        low = (w - high.astype(F32)).astype(BF16)
-        wide_ref[span, :] = jnp.concatenate([high, low], axis=1)
+        offsets.insert(0, later)
+        later = later + sums[b * heads : (b + 1) * heads]
+    w = turn_over(jnp.exp(after + jnp.concatenate(offsets, axis=0)) * tall_steps)
+    for b in range(blocks):
+        block_w = w[:, b * heads : (b + 1) * heads]
+        high = block_w.astype(BF16)
+        low = (block_w - high.astype(F32)).astype(BF16)
+        wide_ref[b * BLOCK : (b + 1) * BLOCK, :] = jnp.concatenate([high, low], axis=1)
     total_logs = jnp.sum(jnp.where(rows == lanes, later, 0.0), axis=0, keepdims=True)
     total_logs = jnp.broadcast_to(total_logs, (PAD, heads))
 
@@ -316,11 +321,12 @@
         )
 
     def scan_copy(s, c):
+        slot = c // 2 + (s - 2) * (chunks // 2) if squared and s > 1 else c
         return remote(
             totals.at[s - 1, c],
             arrived.at[s - 1, c],
             scan_ssems.at[s - 1],
-            scan_rsems.at[s - 1, c],
+            scan_rsems.at[s - 1 if not squared or s == 1 else 1, slot],
             {"ctx": mate(1 if squared and s == 3 else s)},
         )
 
@@ -382,12 +388,14 @@
         if q:
             state_of(q)
         pair_copy(q).start()
+        if q == 0:
+            for copy in late_copies:
+                copy.start()
         if q == 1:
             exchange_logs(0)
-        if q > 1:
-            pair_group(q - 2)
-    for q in range(groups - 2, groups):
-        pair_group(q)
+        if q:
+            pair_group(q - 1)
+    pair_group(groups - 1)
     if squared:
         for c in range(0, chunks, 2):
 
@@ -1010,7 +1018,7 @@
             dma((1,)),
             dma((chunks // GROUP,)),
             dma((scan_steps,)),
-            dma((scan_steps, chunks)),
+            dma((2 if levels == 2 else levels, chunks)),
             dma((1,)),
             dma((1,)),
             dma((1,)),

time: 95.9 us -> 95.2 us (level)
  no operation moved by 1% of the time
where the time goes in v7:
time: 95.2 us; the launch traced here: 94.9 us
  Pallas kernels  94.1 us (99%)
    pallas_call x1, Pallas kernels, per_device(): pl.pallas_call(functools.partial(layer_kernel, dim, n, peers), out_shape=...  92.1 us
    pallas_call x1, Pallas kernels, per_device(): pl.pallas_call(functools.partial(hand_over_kernel, bands), out_shape=(sha...  2 us

profile of v7, /device:TPU:21, one launch (start us, length us, event | category | flops | bytes accessed | tf_op | source)
XLA Modules:
  0.0 94.9 jit_solution(4940632712462272621)
XLA Ops:
  0.6 92.1 %shard_map.158 = (bf16[1024,512]{1,0:T(8,128)(2,1)}, bf16[2,1024]{1,0:T(2,128)(2,1)}) custom-call(s32[2]{0:T(128)} %length_ref.1, bf16[512,2048]{1,0:T(8,128)(2,1)} %values_hbm.1, bf16[512,2048]{1,0:T(8,128)(2,1)} %gate_hbm.1, bf16[512,256]{1,0:T(8,128)(2,1)} %bitcast.9, bf16[512,256]{1,0:T(8,128)(2,1)} %bitcast.10, f32[32,512]{1,0:T(8,128)} %step_ref.1, ...), custom_call_target="tpu_custom_call" | custom-call | tf_op jit(solution)/shard_map/pallas_call | solution.py:945
  92.8 2.0 %shard_map.159 = (bf16[1024,512]{1,0:T(8,128)(2,1)}, bf16[2,1024]{1,0:T(2,128)(2,1)}) custom-call(bf16[1024,512]{1,0:T(8,128)(2,1)} %get-tuple-element.6.mixed_hbm, bf16[2,1024]{1,0:T(2,128)(2,1)} %get-tuple-element.7.smixed_hbm), custom_call_target="tpu_custom_call" | custom-call | tf_op jit(solution)/shard_map/pallas_call | solution.py:1055

commit v8 on v7

--- a/solution.py
+++ b/solution.py
@@ -53,8 +53,8 @@
     return (total * lax.rsqrt(mean + 1e-05) * weight).astype(BF16)
 
 
-CHUNK = LANES
-GROUP = 4
+CHUNK = 2 * LANES
+GROUP = 2
 PARTS = 2
 LAG = 3
 HOOKS = 4
@@ -455,7 +455,7 @@
         first = [(q, cross_row, q) for q in range(pairs)]
         first += [(q + pairs, end_row, q) for q in range(pairs)]
         second = [(q, next_row, q) for q in range(pairs)]
-        second += [(q + 4.5, last_column, q) for q in range(pairs)]
+        second += [(q + 2.5, last_column, q) for q in range(pairs)]
         return [sorted(events, key=lambda event: event[0]) for events in (first, second)]
 
     def run_events(here, events):

time: 95.2 us -> 95 us (level)
  no operation moved by 1% of the time
where the time goes in v8:
time: 95 us; the launch traced here: 94.8 us
  Pallas kernels  94.1 us (99%)
    pallas_call x1, Pallas kernels, per_device(): pl.pallas_call(functools.partial(layer_kernel, dim, n, peers), out_shape=...  92.1 us
    pallas_call x1, Pallas kernels, per_device(): pl.pallas_call(functools.partial(hand_over_kernel, bands), out_shape=(sha...  2 us

profile of v8, /device:TPU:21, one launch (start us, length us, event | category | flops | bytes accessed | tf_op | source)
XLA Modules:
  0.0 94.8 jit_solution(9153961063804628776)
XLA Ops:
  0.6 92.1 %shard_map.158 = (bf16[1024,512]{1,0:T(8,128)(2,1)}, bf16[2,1024]{1,0:T(2,128)(2,1)}) custom-call(s32[2]{0:T(128)} %length_ref.1, bf16[512,2048]{1,0:T(8,128)(2,1)} %values_hbm.1, bf16[512,2048]{1,0:T(8,128)(2,1)} %gate_hbm.1, bf16[512,256]{1,0:T(8,128)(2,1)} %bitcast.9, bf16[512,256]{1,0:T(8,128)(2,1)} %bitcast.10, f32[32,512]{1,0:T(8,128)} %step_ref.1, ...), custom_call_target="tpu_custom_call" | custom-call | tf_op jit(solution)/shard_map/pallas_call | solution.py:945
  92.8 2.0 %shard_map.159 = (bf16[1024,512]{1,0:T(8,128)(2,1)}, bf16[2,1024]{1,0:T(2,128)(2,1)}) custom-call(bf16[1024,512]{1,0:T(8,128)(2,1)} %get-tuple-element.6.mixed_hbm, bf16[2,1024]{1,0:T(2,128)(2,1)} %get-tuple-element.7.smixed_hbm), custom_call_target="tpu_custom_call" | custom-call | tf_op jit(solution)/shard_map/pallas_call | solution.py:1055

commit v9 on v7

--- a/solution.py
+++ b/solution.py
@@ -199,8 +199,7 @@
 
     tile_copy = pltpu.make_async_copy(weight_hbm, tiles_ref, tile_sems.at[0])
 
-    for q in range(groups):
-        value_copy(q).start()
+    value_copy(0).start()
 
     def digit(s):
         return (seat // (1 << s)) % 2
@@ -269,6 +268,9 @@
         wide_ref[b * BLOCK : (b + 1) * BLOCK, :] = jnp.concatenate([high, low], axis=1)
     total_logs = jnp.sum(jnp.where(rows == lanes, later, 0.0), axis=0, keepdims=True)
     total_logs = jnp.broadcast_to(total_logs, (PAD, heads))
+
+    for q in range(1, groups):
+        value_copy(q).start()
 
     def turn_inject():
         turned_ref[...] = turn_over(inject_ref[...].astype(F32)).astype(BF16)

time: 95.2 us -> 95.1 us (level)
  no operation moved by 1% of the time
where the time goes in v9:
time: 95.1 us; the launch traced here: 94.9 us
  Pallas kernels  94.1 us (99%)
    pallas_call x1, Pallas kernels, per_device(): pl.pallas_call(functools.partial(layer_kernel, dim, n, peers), out_shape=...  92.1 us
    pallas_call x1, Pallas kernels, per_device(): pl.pallas_call(functools.partial(hand_over_kernel, bands), out_shape=(sha...  2 us

profile of v9, /device:TPU:21, one launch (start us, length us, event | category | flops | bytes accessed | tf_op | source)
XLA Modules:
  0.0 94.9 jit_solution(4912202988965090064)
XLA Ops:
  0.6 92.1 %shard_map.158 = (bf16[1024,512]{1,0:T(8,128)(2,1)}, bf16[2,1024]{1,0:T(2,128)(2,1)}) custom-call(s32[2]{0:T(128)} %length_ref.1, bf16[512,2048]{1,0:T(8,128)(2,1)} %values_hbm.1, bf16[512,2048]{1,0:T(8,128)(2,1)} %gate_hbm.1, bf16[512,256]{1,0:T(8,128)(2,1)} %bitcast.9, bf16[512,256]{1,0:T(8,128)(2,1)} %bitcast.10, f32[32,512]{1,0:T(8,128)} %step_ref.1, ...), custom_call_target="tpu_custom_call" | custom-call | tf_op jit(solution)/shard_map/pallas_call | solution.py:947
  92.8 2.0 %shard_map.159 = (bf16[1024,512]{1,0:T(8,128)(2,1)}, bf16[2,1024]{1,0:T(2,128)(2,1)}) custom-call(bf16[1024,512]{1,0:T(8,128)(2,1)} %get-tuple-element.6.mixed_hbm, bf16[2,1024]{1,0:T(2,128)(2,1)} %get-tuple-element.7.smixed_hbm), custom_call_target="tpu_custom_call" | custom-call | tf_op jit(solution)/shard_map/pallas_call | solution.py:1057
